TPU v7x, 32 devices: a whole 2x2x4 slice. The times are simulated.
32 devices in a mesh: blk: 4 (over y, x), head: 8 (over z, core).
Axes of the slice: x: 2, y: 2, z: 4, core: 2. Of those that a mesh axis runs over, the one named last changes fastest.
Arguments:
- queries: bfloat16 [2048, 12288], P(('blk', 'head')), may hold values from -64 to 64, as said below
- exponents: int32 [2048, 64], P(('blk', 'head')), may hold values from -2 to 2
- latent: bfloat16 [2048, 576], P(('blk', 'head')), may hold values from -6 to 6, as said below
- segments: int32 [2048], P(('blk', 'head')), may hold values from 0 to 11, never falling along the last dimension, each value on 1 to 256 neighbouring positions
- key_weight: bfloat16 [512, 8192], P(None, 'head'), may hold values from -0.25 to 0.25
- value_weight: bfloat16 [512, 8192], P(None, 'head'), may hold values from -0.25 to 0.25
Outputs:
- attended: bfloat16 [2048, 8192], P(('blk', 'head'))
Inputs may be any that keep to these rules, and one draw needn't show every extreme that they name: queries stay within the range. `latent`: latents stay within the range. `segments`: document numbers never fall along the sequence, and a document holds at most 256 tokens.
All inputs are finite; a program needn't handle non-finite values.
Results may differ from a plain program's by a relative error of at most 0.0069.
Values may be sent and summed in bfloat16 or wider, within the bound.
No kernel may reach another device: no remote copies, remote signals or barrier semaphores. Data moves between devices by JAX's collectives and lax.ppermute only.
A program may use at most 64 MiB of HBM per device.

v0:
```python
import functools
import math

import jax
import jax.numpy as jnp
from jax import lax
from jax.experimental import pallas as pl
from jax.experimental.pallas import tpu as pltpu
from jax.sharding import PartitionSpec as P


NOPE = 128
ROPE = 64
LATENT = 512
VDIM = 128
LANES = 128
MINUS = -1e30
GRANT = 16 * 1024 * 1024


def power_two(exponent):
    result = jnp.zeros(exponent.shape, jnp.float32)
    for level in range(-4, 5):
        result = result + jnp.where(exponent == level, jnp.float32(2.0**level), jnp.float32(0.0))
    return result


def scale_part(distances, local, scal, queries, exponents, outs):
    rows = queries.shape[0]
    heads = exponents.shape[1]
    width = local * (NOPE + ROPE)
    powers = power_two(exponents[...]).astype(jnp.bfloat16)
    lane = lax.broadcasted_iota(jnp.int32, (rows, LANES), 1)
    low = lane < ROPE
    from_head = lax.broadcasted_iota(jnp.int32, (heads, local * LANES), 0)
    to_head = lax.broadcasted_iota(jnp.int32, (heads, local * LANES), 1) // LANES
    for distance, out in zip(distances, outs):
        target = scal[0] ^ distance
        spread = jnp.where(from_head == to_head + target * local, 1.0, 0.0).astype(jnp.bfloat16)
        factor = jnp.dot(powers, spread, preferred_element_type=jnp.float32)
        first = pl.multiple_of(target * width, LANES)
        for pair in range(local // 2):
            base = pair * 3 * LANES
            one, two, three = (
                queries[:, pl.ds(first + base + k * LANES, LANES)].astype(jnp.float32) for k in range(3)
            )
            even = factor[:, 2 * pair * LANES : (2 * pair + 1) * LANES]
            odd = factor[:, (2 * pair + 1) * LANES : (2 * pair + 2) * LANES]
            nope_odd = pltpu.roll(jnp.where(low, three, two), ROPE, 1)
            ropes = jnp.where(low, two, three) * jnp.where(low, even, odd)
            at = 2 * pair * LANES
            out[:, at : at + LANES] = (one * even).astype(jnp.bfloat16)
            out[:, at + LANES : at + 2 * LANES] = (nope_odd * odd).astype(jnp.bfloat16)
            at = (local + pair) * LANES
            out[:, at : at + LANES] = ropes.astype(jnp.bfloat16)


def latent_part(latent, segments, out):
    rows = latent.shape[0]
    width = LATENT + ROPE
    square = lax.broadcasted_iota(jnp.int32, (rows, rows), 0) == lax.broadcasted_iota(jnp.int32, (rows, rows), 1)
    column = jnp.sum(jnp.where(square, segments[...].astype(jnp.float32), 0.0), axis=1, keepdims=True) + 1.0
    lane = lax.broadcasted_iota(jnp.int32, (rows, ROPE), 1)
    out[:, :width] = latent[...]
    out[:, width:] = jnp.where(lane == 0, column, 0.0).astype(jnp.bfloat16)


def prepare_kernel(distances, local, scal, queries, exponents, latent, segments, padded, *outs):
    latent_part(latent, segments, padded)
    scale_part(distances, local, scal, queries, exponents, outs)


def scale_kernel(distances, local, scal, queries, exponents, *outs):
    scale_part(distances, local, scal, queries, exponents, outs)


def project_kernel(rows, chips, scal, mine, theirs, key_weight, value_weight, keys, values, tail, window):
    place, core = scal[0] // 2, scal[0] % 2
    lead = chips * rows
    other_half = jnp.where(place < chips // 2, chips // 2, 0)
    for slot in range(chips + chips // 2):
        if slot < chips:
            to = lead + (place ^ slot) * 2 * rows
        else:
            to = ((place ^ (other_half + slot - chips)) - chips // 2) * 2 * rows
        take = slice(slot * rows, (slot + 1) * rows)
        window[pl.ds(pl.multiple_of(to + core * rows, rows), rows), :] = mine[take, :]
        window[pl.ds(pl.multiple_of(to + (1 - core) * rows, rows), rows), :] = theirs[take, :]
    tail[...] = window[:, LATENT:]
    columns = keys.shape[1]
    tile = min(256, columns)
    step_rows = 256

    def one(step, carry):
        at = pl.multiple_of(step * tile, tile)
        for start in range(0, window.shape[0], step_rows):
            part = window[start : start + step_rows, :LATENT]
            for weight, out in ((key_weight, keys), (value_weight, values)):
                out[start : start + step_rows, pl.ds(at, tile)] = jnp.dot(
                    part, weight[:, pl.ds(at, tile)], preferred_element_type=jnp.float32
                ).astype(jnp.bfloat16)
        return carry

    lax.fori_loop(0, columns // tile, one, 0)


def attend_kernel(rows, chips, local, slot, scal, mine, theirs, keys, values, tail, out_mine, out_theirs):
    place, core = scal[0] // 2, scal[0] % 2
    lead = chips * rows
    chip = place ^ slot
    block = 2 * rows
    width = lead + block
    start = pl.multiple_of(chip * block, block)
    own = pl.multiple_of(lead + start + core * rows, rows)
    other = pl.multiple_of(lead + start + (1 - core) * rows, rows)
    key_tail = tail[pl.ds(start, width), :]
    pick = jnp.where(lax.broadcasted_iota(jnp.int32, (8, LANES), 1) == ROPE, 1.0, 0.0).astype(jnp.bfloat16)
    key_seg = lax.dot_general(pick, key_tail, (((1,), (1,)), ((), ())), preferred_element_type=jnp.float32)[0:1]
    query_tail = jnp.concatenate([tail[pl.ds(own, rows), :], tail[pl.ds(other, rows), :]], axis=0)
    query_seg = query_tail[:, ROPE : ROPE + 1].astype(jnp.float32)
    row = lax.broadcasted_iota(jnp.int32, (block, width), 0)
    column = lax.broadcasted_iota(jnp.int32, (block, width), 1)
    shift = jnp.where(row < rows, core * rows, -core * rows)
    bias = jnp.where((query_seg == key_seg) & (column <= row + shift + lead), 0.0, MINUS)
    lane = lax.broadcasted_iota(jnp.int32, (width, LANES), 1)
    rope_even = jnp.where(lane < ROPE, key_tail.astype(jnp.float32), 0.0)
    rope_odd = pltpu.roll(rope_even, ROPE, 1)
    rope = (rope_even.astype(jnp.bfloat16), rope_odd.astype(jnp.bfloat16))
    factor = math.log2(math.e) / math.sqrt(NOPE + ROPE)
    for head in range(local):
        at = slice(head * LANES, (head + 1) * LANES)
        pair = slice((local + head // 2) * LANES, (local + head // 2 + 1) * LANES)
        query = jnp.concatenate(
            [
                jnp.concatenate([mine[:, at], mine[:, pair]], axis=1),
                jnp.concatenate([theirs[:, at], theirs[:, pair]], axis=1),
            ],
            axis=0,
        )
        key = jnp.concatenate([keys[pl.ds(start, width), at], rope[head % 2]], axis=1)
        scores = lax.dot_general(query, key, (((1,), (1,)), ((), ())), preferred_element_type=jnp.float32)
        scores = scores * factor + bias
        largest = jnp.max(scores, axis=1, keepdims=True)
        weights = jnp.exp2(scores - largest)
        inverse = 1.0 / jnp.sum(weights, axis=1, keepdims=True)
        weighted = jnp.dot(
            weights.astype(jnp.bfloat16), values[pl.ds(start, width), at], preferred_element_type=jnp.float32
        )
        result = (weighted * inverse).astype(jnp.bfloat16)
        out_mine[:, at] = result[:rows]
        out_theirs[:, at] = result[rows:]


def join_kernel(scal, *refs):
    pieces, out = refs[:-1], refs[-1]
    width = pieces[0].shape[1]
    for distance, piece in enumerate(pieces):
        out[:, pl.ds(pl.multiple_of((scal[0] ^ distance) * width, LANES), width)] = piece[...]


def call(kernel, outs, *args, scratch=(), flops=0, nbytes=0, exps=0):
    vmem = pl.BlockSpec(memory_space=pltpu.VMEM)
    smem = pl.BlockSpec(memory_space=pltpu.SMEM)
    specs = [smem] + [vmem] * (len(args) - 1)
    shapes = [jax.ShapeDtypeStruct(shape, jnp.bfloat16) for shape in outs]
    return pl.pallas_call(
        kernel,
        out_shape=shapes,
        in_specs=specs,
        out_specs=[vmem] * len(outs),
        scratch_shapes=list(scratch),
        cost_estimate=pl.CostEstimate(flops=flops, bytes_accessed=nbytes, transcendentals=exps),
        compiler_params=pltpu.CompilerParams(vmem_limit_bytes=GRANT),
    )(*args)


def layer(queries, exponents, latent, segments, key_weight, value_weight):
    rows = queries.shape[0]
    heads = exponents.shape[1]
    count = lax.axis_size("head")
    blocks = lax.axis_size("blk")
    local = heads // count
    width = queries.shape[1] // count
    chips = count // 2
    lead = chips * rows
    window_rows = 3 * lead
    columns = local * VDIM
    position = lax.axis_index("head").astype(jnp.int32)
    scal = position.reshape(1)

    def swap(block, distance):
        return lax.ppermute(block, "head", [(i, i ^ distance) for i in range(count)])

    far = list(range(chips, count))
    near = list(range(chips))
    piece = (rows, width)
    padded, *far_pieces = call(
        functools.partial(prepare_kernel, far, local),
        [(rows, LATENT + 2 * ROPE)] + [piece] * len(far),
        scal,
        queries,
        exponents,
        latent,
        segments.reshape(1, rows),
        nbytes=2000000,
    )
    near_pieces = call(
        functools.partial(scale_kernel, near, local), [piece] * len(near), scal, queries, exponents, nbytes=2000000
    )
    sent = list(near_pieces) + list(far_pieces)

    own = [padded] + [swap(padded, 2 * k) for k in range(1, chips)]
    own = jnp.concatenate(own, axis=0)
    other_half = jnp.where(position // 2 < chips // 2, chips // 2, 0)
    upper = lax.dynamic_slice_in_dim(own, other_half * rows, chips // 2 * rows, 0)
    earlier = lax.ppermute(upper, "blk", [(i, i + 1) for i in range(blocks - 1)])
    mine = jnp.concatenate([own, earlier], axis=0)
    theirs = swap(mine, 1)

    arrived = [sent[0]] + [swap(sent[distance], distance) for distance in range(1, count)]

    keys, values, tail = call(
        functools.partial(project_kernel, rows, chips),
        [(window_rows, columns), (window_rows, columns), (window_rows, LANES)],
        scal,
        mine,
        theirs,
        key_weight,
        value_weight,
        scratch=[pltpu.VMEM((window_rows, LATENT + LANES), jnp.bfloat16)],
        flops=4 * window_rows * LATENT * columns,
        nbytes=4 * LATENT * columns,
    )

    returned = [None] * count
    span = lead + 2 * rows
    for slot in range(chips):
        results = call(
            functools.partial(attend_kernel, rows, chips, local, slot),
            [(rows, columns)] * 2,
            scal,
            arrived[2 * slot],
            arrived[2 * slot + 1],
            keys,
            values,
            tail,
            flops=2 * 2 * rows * span * local * 384,
            nbytes=4 * rows * (width + columns),
            exps=2 * rows * span * local,
        )
        for distance, result in zip((2 * slot, 2 * slot + 1), results):
            returned[distance] = result if distance == 0 else swap(result, distance)
    (joined,) = call(join_kernel, [(rows, heads * VDIM)], scal, *returned, nbytes=4 * rows * heads * VDIM)
    return joined


def solution(mesh):
    in_specs = (
        P(("blk", "head"), None),
        P(("blk", "head"), None),
        P(("blk", "head"), None),
        P(("blk", "head")),
        P(None, "head"),
        P(None, "head"),
    )
    out_specs = P(("blk", "head"), None)
    return jax.shard_map(layer, mesh=mesh, in_specs=in_specs, out_specs=out_specs, check_vma=False)
```

profile of v0, /device:TPU:0, one launch (start us, length us, event | category | flops | bytes accessed | tf_op | source)
XLA Modules:
  0.0 90.2 jit_solution(7998169072621217665)
XLA Ops:
  0.0 1.4 %copy-done = bf16[64,12288]{1,0:T(8,128)(2,1)S(1)} copy-done((bf16[64,12288]{1,0:T(8,128)(2,1)S(1)}, bf16[64,12288]{1,0:T(8,128)(2,1)}, u32[]{:S(2)}) %copy-start) | copy-done | bytes 1572888
  4.2 3.1 %collective-permute-start.1 = (bf16[64,640]{1,0:T(8,128)(2,1)S(1)}, bf16[64,640]{1,0:T(8,128)(2,1)}, u32[]{:S(2)}, u32[]{:S(2)}) collective-permute-start(bf16[64,640]{1,0:T(8,128)(2,1)S(1)} %get-tuple-element.27), channel_id=1, source_target_pairs={{0,2},{1,3},{2,0},{3,1},{4,6},{5,7},{6,4},{7,5},{8,10},{9,11},{10,... | collective-permute-start | bytes 245768 | tf_op jit(solution)/shard_map/ppermute | solution.py:192
  7.3 2.6 %collective-permute-start.2 = (bf16[64,640]{1,0:T(8,128)(2,1)S(1)}, bf16[64,640]{1,0:T(8,128)(2,1)}, u32[]{:S(2)}, u32[]{:S(2)}) collective-permute-start(bf16[64,640]{1,0:T(8,128)(2,1)S(1)} %get-tuple-element.27), channel_id=1, source_target_pairs={{0,4},{1,5},{2,6},{3,7},{4,0},{5,1},{6,2},{7,3},{8,12},{9,13},{10,... | collective-permute-start | bytes 245768 | tf_op jit(solution)/shard_map/ppermute | solution.py:192
  9.9 6.7 %collective-permute-done.2 = bf16[64,640]{1,0:T(8,128)(2,1)} collective-permute-done((bf16[64,640]{1,0:T(8,128)(2,1)S(1)}, bf16[64,640]{1,0:T(8,128)(2,1)}, u32[]{:S(2)}, u32[]{:S(2)}) %collective-permute-start.2) | collective-permute-done | bytes 81952 | tf_op jit(solution)/shard_map/ppermute | solution.py:192
  17.7 3.4 %collective-permute-start.4 = (bf16[128,640]{1,0:T(8,128)(2,1)S(1)}, bf16[128,640]{1,0:T(8,128)(2,1)S(1)}, u32[]{:S(2)}, u32[]{:S(2)}) collective-permute-start(bf16[128,640]{1,0:T(8,128)(2,1)S(1)} %fusion.2), channel_id=1, source_target_pairs={{0,8},{8,16},{16,24},{1,9},{9,17},{17,25},{2,10},{10,18},{18,26},{... | collective-permute-start | bytes 491528 | tf_op jit(solution)/shard_map/ppermute | solution.py:216
  24.0 2.5 %collective-permute-start.15 = (bf16[64,1536]{1,0:T(8,128)(2,1)S(1)}, bf16[64,1536]{1,0:T(8,128)(2,1)S(1)}, u32[]{:S(2)}, u32[]{:S(2)}) collective-permute-start(bf16[64,1536]{1,0:T(8,128)(2,1)S(1)} %get-tuple-element.41), channel_id=1, source_target_pairs={{0,6},{1,7},{2,4},{3,5},{4,2},{5,3},{6,0},{7,1},{8,14},{9,15},{10,... | collective-permute-start | bytes 589832 | tf_op jit(solution)/shard_map/ppermute | solution.py:192
  26.6 1.1 %collective-permute-start.16 = (bf16[64,1536]{1,0:T(8,128)(2,1)S(1)}, bf16[64,1536]{1,0:T(8,128)(2,1)S(1)}, u32[]{:S(2)}, u32[]{:S(2)}) collective-permute-start(bf16[64,1536]{1,0:T(8,128)(2,1)S(1)} %get-tuple-element.42), channel_id=1, source_target_pairs={{0,7},{1,6},{2,5},{3,4},{4,3},{5,2},{6,1},{7,0},{8,15},{9,14},{10,... | collective-permute-start | bytes 589832 | tf_op jit(solution)/shard_map/ppermute | solution.py:192
  28.3 2.0 %collective-permute-start.12 = (bf16[64,1536]{1,0:T(8,128)(2,1)S(1)}, bf16[64,1536]{1,0:T(8,128)(2,1)S(1)}, u32[]{:S(2)}, u32[]{:S(2)}) collective-permute-start(bf16[64,1536]{1,0:T(8,128)(2,1)S(1)} %get-tuple-element.38), channel_id=1, source_target_pairs={{0,5},{1,4},{2,7},{3,6},{4,1},{5,0},{6,3},{7,2},{8,13},{9,12},{10,... | collective-permute-start | bytes 589832 | tf_op jit(solution)/shard_map/ppermute | solution.py:192
  30.8 3.0 %collective-permute-done.15.mine = bf16[64,1536]{1,0:T(8,128)(2,1)S(1)} collective-permute-done((bf16[64,1536]{1,0:T(8,128)(2,1)S(1)}, bf16[64,1536]{1,0:T(8,128)(2,1)S(1)}, u32[]{:S(2)}, u32[]{:S(2)}) %collective-permute-start.15) | collective-permute-done | bytes 196640 | tf_op jit(solution)/shard_map/ppermute | solution.py:192
  33.8 16.4 %collective-permute-start.7 = (bf16[64,1536]{1,0:T(8,128)(2,1)S(1)}, bf16[64,1536]{1,0:T(8,128)(2,1)S(1)}, u32[]{:S(2)}, u32[]{:S(2)}) collective-permute-start(bf16[64,1536]{1,0:T(8,128)(2,1)S(1)} %get-tuple-element.33), channel_id=1, source_target_pairs={{0,2},{1,3},{2,0},{3,1},{4,6},{5,7},{6,4},{7,5},{8,10},{9,11},{10,... | collective-permute-start | bytes 589832 | tf_op jit(solution)/shard_map/ppermute | solution.py:192
  50.2 3.9 %collective-permute-start.8 = (bf16[64,1536]{1,0:T(8,128)(2,1)S(1)}, bf16[64,1536]{1,0:T(8,128)(2,1)S(1)}, u32[]{:S(2)}, u32[]{:S(2)}) collective-permute-start(bf16[64,1536]{1,0:T(8,128)(2,1)S(1)} %get-tuple-element.34), channel_id=1, source_target_pairs={{0,3},{1,2},{2,1},{3,0},{4,7},{5,6},{6,5},{7,4},{8,11},{9,10},{10,... | collective-permute-start | bytes 589832 | tf_op jit(solution)/shard_map/ppermute | solution.py:192
  54.1 2.5 %shard_map.66 = (bf16[768,1024]{1,0:T(8,128)(2,1)S(1)}, bf16[768,1024]{1,0:T(8,128)(2,1)S(1)}, bf16[768,128]{1,0:T(8,128)(2,1)S(1)}) custom-call(s32[1]{0:T(128)} %bitcast.scal, bf16[384,640]{1,0:T(8,128)(2,1)S(1)} %constant_dynamic-update-slice_fusion.mine, bf16[384,640]{1,0:T(8,128)(2,1)S(1)} %collective-permute-done.5.theirs, ...), custom_call_target="tpu_custom_call" | custom-call | flops 1610612736 | bytes 2097152 | tf_op jit(solution)/shard_map/pallas_call | solution.py:166
  56.7 2.5 %shard_map.70 = (bf16[64,1024]{1,0:T(8,128)(2,1)S(1)}, bf16[64,1024]{1,0:T(8,128)(2,1)S(1)}) custom-call(s32[1]{0:T(128)} %bitcast.scal, bf16[64,1536]{1,0:T(8,128)(2,1)S(1)} %collective-permute-done.15.mine, bf16[64,1536]{1,0:T(8,128)(2,1)S(1)} %collective-permute-done.16.theirs, bf16[768,1024]{1,0:T(8,128)(2,1)S(1)} %get-tuple-element.28.keys, ...), custom_call_target="tpu_custom_call" | custom-call | flops 301989888 | bytes 655360 | tf_op jit(solution)/shard_map/pallas_call | solution.py:166
  59.2 2.5 %collective-permute-start.17 = (bf16[64,1024]{1,0:T(8,128)(2,1)S(1)}, bf16[64,1024]{1,0:T(8,128)(2,1)S(1)}, u32[]{:S(2)}, u32[]{:S(2)}) collective-permute-start(bf16[64,1024]{1,0:T(8,128)(2,1)S(1)} %get-tuple-element.43), channel_id=1, source_target_pairs={{0,6},{1,7},{2,4},{3,5},{4,2},{5,3},{6,0},{7,1},{8,14},{9,15},{10,... | collective-permute-start | bytes 393224 | tf_op jit(solution)/shard_map/ppermute | solution.py:192
  61.7 2.0 %collective-permute-start.18 = (bf16[64,1024]{1,0:T(8,128)(2,1)S(1)}, bf16[64,1024]{1,0:T(8,128)(2,1)S(1)}, u32[]{:S(2)}, u32[]{:S(2)}) collective-permute-start(bf16[64,1024]{1,0:T(8,128)(2,1)S(1)} %get-tuple-element.44), channel_id=1, source_target_pairs={{0,7},{1,6},{2,5},{3,4},{4,3},{5,2},{6,1},{7,0},{8,15},{9,14},{10,... | collective-permute-start | bytes 393224 | tf_op jit(solution)/shard_map/ppermute | solution.py:192
  63.7 2.5 %shard_map.69 = (bf16[64,1024]{1,0:T(8,128)(2,1)S(1)}, bf16[64,1024]{1,0:T(8,128)(2,1)S(1)}) custom-call(s32[1]{0:T(128)} %bitcast.scal, bf16[64,1536]{1,0:T(8,128)(2,1)S(1)} %collective-permute-done.11.mine, bf16[64,1536]{1,0:T(8,128)(2,1)S(1)} %collective-permute-done.12.theirs, bf16[768,1024]{1,0:T(8,128)(2,1)S(1)} %get-tuple-element.28.keys, ...), custom_call_target="tpu_custom_call" | custom-call | flops 301989888 | bytes 655360 | tf_op jit(solution)/shard_map/pallas_call | solution.py:166
  66.3 5.3 %collective-permute-done.8.theirs = bf16[64,1536]{1,0:T(8,128)(2,1)S(1)} collective-permute-done((bf16[64,1536]{1,0:T(8,128)(2,1)S(1)}, bf16[64,1536]{1,0:T(8,128)(2,1)S(1)}, u32[]{:S(2)}, u32[]{:S(2)}) %collective-permute-start.8) | collective-permute-done | bytes 196640 | tf_op jit(solution)/shard_map/ppermute | solution.py:192
  71.9 2.5 %shard_map.68 = (bf16[64,1024]{1,0:T(8,128)(2,1)S(1)}, bf16[64,1024]{1,0:T(8,128)(2,1)S(1)}) custom-call(s32[1]{0:T(128)} %bitcast.scal, bf16[64,1536]{1,0:T(8,128)(2,1)S(1)} %collective-permute-done.7.mine, bf16[64,1536]{1,0:T(8,128)(2,1)S(1)} %collective-permute-done.8.theirs, bf16[768,1024]{1,0:T(8,128)(2,1)S(1)} %get-tuple-element.28.keys, ...), custom_call_target="tpu_custom_call" | custom-call | flops 301989888 | bytes 655360 | tf_op jit(solution)/shard_map/pallas_call | solution.py:166
  74.4 2.5 %collective-permute-start.10 = (bf16[64,1024]{1,0:T(8,128)(2,1)S(1)}, bf16[64,1024]{1,0:T(8,128)(2,1)S(1)}, u32[]{:S(2)}, u32[]{:S(2)}) collective-permute-start(bf16[64,1024]{1,0:T(8,128)(2,1)S(1)} %get-tuple-element.36), channel_id=1, source_target_pairs={{0,3},{1,2},{2,1},{3,0},{4,7},{5,6},{6,5},{7,4},{8,11},{9,10},{10,... | collective-permute-start | bytes 393224 | tf_op jit(solution)/shard_map/ppermute | solution.py:192
  77.0 2.5 %shard_map.67 = (bf16[64,1024]{1,0:T(8,128)(2,1)S(1)}, bf16[64,1024]{1,0:T(8,128)(2,1)S(1)}) custom-call(s32[1]{0:T(128)} %bitcast.scal, bf16[64,1536]{1,0:T(8,128)(2,1)S(1)} %get-tuple-element.25.mine, bf16[64,1536]{1,0:T(8,128)(2,1)S(1)} %collective-permute-done.theirs, bf16[768,1024]{1,0:T(8,128)(2,1)S(1)} %get-tuple-element.28.keys, ...), custom_call_target="tpu_custom_call" | custom-call | flops 301989888 | bytes 655360 | tf_op jit(solution)/shard_map/pallas_call | solution.py:166
  80.4 1.9 %collective-permute-done.13.refs_4_ = bf16[64,1024]{1,0:T(8,128)(2,1)S(1)} collective-permute-done((bf16[64,1024]{1,0:T(8,128)(2,1)S(1)}, bf16[64,1024]{1,0:T(8,128)(2,1)S(1)}, u32[]{:S(2)}, u32[]{:S(2)}) %collective-permute-start.13) | collective-permute-done | bytes 131104 | tf_op jit(solution)/shard_map/ppermute | solution.py:192
  82.3 1.3 %collective-permute-done.14.refs_5_ = bf16[64,1024]{1,0:T(8,128)(2,1)S(1)} collective-permute-done((bf16[64,1024]{1,0:T(8,128)(2,1)S(1)}, bf16[64,1024]{1,0:T(8,128)(2,1)S(1)}, u32[]{:S(2)}, u32[]{:S(2)}) %collective-permute-start.14) | collective-permute-done | bytes 131104 | tf_op jit(solution)/shard_map/ppermute | solution.py:192
  83.6 2.1 %collective-permute-done.10.refs_3_ = bf16[64,1024]{1,0:T(8,128)(2,1)S(1)} collective-permute-done((bf16[64,1024]{1,0:T(8,128)(2,1)S(1)}, bf16[64,1024]{1,0:T(8,128)(2,1)S(1)}, u32[]{:S(2)}, u32[]{:S(2)}) %collective-permute-start.10) | collective-permute-done | bytes 131104 | tf_op jit(solution)/shard_map/ppermute | solution.py:192
  85.7 3.4 %collective-permute-done.9.refs_2_ = bf16[64,1024]{1,0:T(8,128)(2,1)S(1)} collective-permute-done((bf16[64,1024]{1,0:T(8,128)(2,1)S(1)}, bf16[64,1024]{1,0:T(8,128)(2,1)S(1)}, u32[]{:S(2)}, u32[]{:S(2)}) %collective-permute-start.9) | collective-permute-done | bytes 131104 | tf_op jit(solution)/shard_map/ppermute | solution.py:192
  (44 shorter events, 10.1 us)
Async XLA Ops:
  0.0 1.4 %copy-start = (bf16[64,12288]{1,0:T(8,128)(2,1)S(1)}, bf16[64,12288]{1,0:T(8,128)(2,1)}, u32[]{:S(2)}) copy-start(bf16[64,12288]{1,0:T(8,128)(2,1)} %queries.3) | copy-start | bytes 4718596
  3.7 26.6 %copy-start.1 = (bf16[64,12288]{1,0:T(8,128)(2,1)S(1)}, bf16[64,12288]{1,0:T(8,128)(2,1)}, u32[]{:S(2)}) copy-start(bf16[64,12288]{1,0:T(8,128)(2,1)} %queries.3) | copy-start | bytes 4718596
  3.7 26.6 %copy-start.3 = (s32[64,64]{1,0:T(8,128)S(1)}, s32[64,64]{1,0:T(8,128)}, u32[]{:S(2)}) copy-start(s32[64,64]{1,0:T(8,128)} %exponents.3) | copy-start | bytes 49156
  4.2 49.9 %copy-start.6 = (bf16[512,1024]{1,0:T(8,128)(2,1)S(1)}, bf16[512,1024]{1,0:T(8,128)(2,1)}, u32[]{:S(2)}) copy-start(bf16[512,1024]{1,0:T(8,128)(2,1)} %key_weight.1) | copy-start | bytes 3145732
  4.2 5.7 %collective-permute-start.1 = (bf16[64,640]{1,0:T(8,128)(2,1)S(1)}, bf16[64,640]{1,0:T(8,128)(2,1)}, u32[]{:S(2)}, u32[]{:S(2)}) collective-permute-start(bf16[64,640]{1,0:T(8,128)(2,1)S(1)} %get-tuple-element.27), channel_id=1, source_target_pairs={{0,2},{1,3},{2,0},{3,1},{4,6},{5,7},{6,4},{7,5},{8,10},{9,11},{10,... | collective-permute-start | bytes 245768 | tf_op jit(solution)/shard_map/ppermute | solution.py:192
  7.3 9.3 %collective-permute-start.2 = (bf16[64,640]{1,0:T(8,128)(2,1)S(1)}, bf16[64,640]{1,0:T(8,128)(2,1)}, u32[]{:S(2)}, u32[]{:S(2)}) collective-permute-start(bf16[64,640]{1,0:T(8,128)(2,1)S(1)} %get-tuple-element.27), channel_id=1, source_target_pairs={{0,4},{1,5},{2,6},{3,7},{4,0},{5,1},{6,2},{7,3},{8,12},{9,13},{10,... | collective-permute-start | bytes 245768 | tf_op jit(solution)/shard_map/ppermute | solution.py:192
  9.9 6.7 %collective-permute-start.3 = (bf16[64,640]{1,0:T(8,128)(2,1)S(1)}, bf16[64,640]{1,0:T(8,128)(2,1)}, u32[]{:S(2)}, u32[]{:S(2)}) collective-permute-start(bf16[64,640]{1,0:T(8,128)(2,1)S(1)} %get-tuple-element.27), channel_id=1, source_target_pairs={{0,6},{1,7},{2,4},{3,5},{4,2},{5,3},{6,0},{7,1},{8,14},{9,15},{10,... | collective-permute-start | bytes 245768 | tf_op jit(solution)/shard_map/ppermute | solution.py:192
  9.9 44.2 %copy-start.7 = (bf16[512,1024]{1,0:T(8,128)(2,1)S(1)}, bf16[512,1024]{1,0:T(8,128)(2,1)}, u32[]{:S(2)}) copy-start(bf16[512,1024]{1,0:T(8,128)(2,1)} %value_weight.1) | copy-start | bytes 3145732
  17.7 6.2 %collective-permute-start.4 = (bf16[128,640]{1,0:T(8,128)(2,1)S(1)}, bf16[128,640]{1,0:T(8,128)(2,1)S(1)}, u32[]{:S(2)}, u32[]{:S(2)}) collective-permute-start(bf16[128,640]{1,0:T(8,128)(2,1)S(1)} %fusion.2), channel_id=1, source_target_pairs={{0,8},{8,16},{16,24},{1,9},{9,17},{17,25},{2,10},{10,18},{18,26},{... | collective-permute-start | bytes 491528 | tf_op jit(solution)/shard_map/ppermute | solution.py:216
  24.0 30.1 %collective-permute-start.5 = (bf16[384,640]{1,0:T(8,128)(2,1)S(1)}, bf16[384,640]{1,0:T(8,128)(2,1)S(1)}, u32[]{:S(2)}, u32[]{:S(2)}) collective-permute-start(bf16[384,640]{1,0:T(8,128)(2,1)S(1)} %constant_dynamic-update-slice_fusion.mine), channel_id=1, source_target_pairs={{0,1},{1,0},{2,3},{3,2},{4,5},{5,4},{6,7},{7,6},{8,9},{9,8},{10,11... | collective-permute-start | bytes 1474568 | tf_op jit(solution)/shard_map/ppermute | solution.py:192
  24.0 9.7 %collective-permute-start.15 = (bf16[64,1536]{1,0:T(8,128)(2,1)S(1)}, bf16[64,1536]{1,0:T(8,128)(2,1)S(1)}, u32[]{:S(2)}, u32[]{:S(2)}) collective-permute-start(bf16[64,1536]{1,0:T(8,128)(2,1)S(1)} %get-tuple-element.41), channel_id=1, source_target_pairs={{0,6},{1,7},{2,4},{3,5},{4,2},{5,3},{6,0},{7,1},{8,14},{9,15},{10,... | collective-permute-start | bytes 589832 | tf_op jit(solution)/shard_map/ppermute | solution.py:192
  26.6 23.6 %collective-permute-start.16 = (bf16[64,1536]{1,0:T(8,128)(2,1)S(1)}, bf16[64,1536]{1,0:T(8,128)(2,1)S(1)}, u32[]{:S(2)}, u32[]{:S(2)}) collective-permute-start(bf16[64,1536]{1,0:T(8,128)(2,1)S(1)} %get-tuple-element.42), channel_id=1, source_target_pairs={{0,7},{1,6},{2,5},{3,4},{4,3},{5,2},{6,1},{7,0},{8,15},{9,14},{10,... | collective-permute-start | bytes 589832 | tf_op jit(solution)/shard_map/ppermute | solution.py:192
  27.7 31.5 %collective-permute-start.11 = (bf16[64,1536]{1,0:T(8,128)(2,1)S(1)}, bf16[64,1536]{1,0:T(8,128)(2,1)S(1)}, u32[]{:S(2)}, u32[]{:S(2)}) collective-permute-start(bf16[64,1536]{1,0:T(8,128)(2,1)S(1)} %get-tuple-element.37), channel_id=1, source_target_pairs={{0,4},{1,5},{2,6},{3,7},{4,0},{5,1},{6,2},{7,3},{8,12},{9,13},{10,... | collective-permute-start | bytes 589832 | tf_op jit(solution)/shard_map/ppermute | solution.py:192
  28.3 33.4 %collective-permute-start.12 = (bf16[64,1536]{1,0:T(8,128)(2,1)S(1)}, bf16[64,1536]{1,0:T(8,128)(2,1)S(1)}, u32[]{:S(2)}, u32[]{:S(2)}) collective-permute-start(bf16[64,1536]{1,0:T(8,128)(2,1)S(1)} %get-tuple-element.38), channel_id=1, source_target_pairs={{0,5},{1,4},{2,7},{3,6},{4,1},{5,0},{6,3},{7,2},{8,13},{9,12},{10,... | collective-permute-start | bytes 589832 | tf_op jit(solution)/shard_map/ppermute | solution.py:192
  33.8 32.4 %collective-permute-start.7 = (bf16[64,1536]{1,0:T(8,128)(2,1)S(1)}, bf16[64,1536]{1,0:T(8,128)(2,1)S(1)}, u32[]{:S(2)}, u32[]{:S(2)}) collective-permute-start(bf16[64,1536]{1,0:T(8,128)(2,1)S(1)} %get-tuple-element.33), channel_id=1, source_target_pairs={{0,2},{1,3},{2,0},{3,1},{4,6},{5,7},{6,4},{7,5},{8,10},{9,11},{10,... | collective-permute-start | bytes 589832 | tf_op jit(solution)/shard_map/ppermute | solution.py:192
  50.2 21.5 %collective-permute-start.8 = (bf16[64,1536]{1,0:T(8,128)(2,1)S(1)}, bf16[64,1536]{1,0:T(8,128)(2,1)S(1)}, u32[]{:S(2)}, u32[]{:S(2)}) collective-permute-start(bf16[64,1536]{1,0:T(8,128)(2,1)S(1)} %get-tuple-element.34), channel_id=1, source_target_pairs={{0,3},{1,2},{2,1},{3,0},{4,7},{5,6},{6,5},{7,4},{8,11},{9,10},{10,... | collective-permute-start | bytes 589832 | tf_op jit(solution)/shard_map/ppermute | solution.py:192
  54.1 20.3 %collective-permute-start = (bf16[64,1536]{1,0:T(8,128)(2,1)S(1)}, bf16[64,1536]{1,0:T(8,128)(2,1)S(1)}, u32[]{:S(2)}, u32[]{:S(2)}) collective-permute-start(bf16[64,1536]{1,0:T(8,128)(2,1)S(1)} %get-tuple-element.26), channel_id=1, source_target_pairs={{0,1},{1,0},{2,3},{3,2},{4,5},{5,4},{6,7},{7,6},{8,9},{9,8},{10,11... | collective-permute-start | bytes 589832 | tf_op jit(solution)/shard_map/ppermute | solution.py:192
  59.2 20.3 %collective-permute-start.17 = (bf16[64,1024]{1,0:T(8,128)(2,1)S(1)}, bf16[64,1024]{1,0:T(8,128)(2,1)S(1)}, u32[]{:S(2)}, u32[]{:S(2)}) collective-permute-start(bf16[64,1024]{1,0:T(8,128)(2,1)S(1)} %get-tuple-element.43), channel_id=1, source_target_pairs={{0,6},{1,7},{2,4},{3,5},{4,2},{5,3},{6,0},{7,1},{8,14},{9,15},{10,... | collective-permute-start | bytes 393224 | tf_op jit(solution)/shard_map/ppermute | solution.py:192
  61.7 18.5 %collective-permute-start.18 = (bf16[64,1024]{1,0:T(8,128)(2,1)S(1)}, bf16[64,1024]{1,0:T(8,128)(2,1)S(1)}, u32[]{:S(2)}, u32[]{:S(2)}) collective-permute-start(bf16[64,1024]{1,0:T(8,128)(2,1)S(1)} %get-tuple-element.44), channel_id=1, source_target_pairs={{0,7},{1,6},{2,5},{3,4},{4,3},{5,2},{6,1},{7,0},{8,15},{9,14},{10,... | collective-permute-start | bytes 393224 | tf_op jit(solution)/shard_map/ppermute | solution.py:192
  66.2 16.1 %collective-permute-start.13 = (bf16[64,1024]{1,0:T(8,128)(2,1)S(1)}, bf16[64,1024]{1,0:T(8,128)(2,1)S(1)}, u32[]{:S(2)}, u32[]{:S(2)}) collective-permute-start(bf16[64,1024]{1,0:T(8,128)(2,1)S(1)} %get-tuple-element.39), channel_id=1, source_target_pairs={{0,4},{1,5},{2,6},{3,7},{4,0},{5,1},{6,2},{7,3},{8,12},{9,13},{10,... | collective-permute-start | bytes 393224 | tf_op jit(solution)/shard_map/ppermute | solution.py:192
  71.6 11.9 %collective-permute-start.14 = (bf16[64,1024]{1,0:T(8,128)(2,1)S(1)}, bf16[64,1024]{1,0:T(8,128)(2,1)S(1)}, u32[]{:S(2)}, u32[]{:S(2)}) collective-permute-start(bf16[64,1024]{1,0:T(8,128)(2,1)S(1)} %get-tuple-element.40), channel_id=1, source_target_pairs={{0,5},{1,4},{2,7},{3,6},{4,1},{5,0},{6,3},{7,2},{8,13},{9,12},{10,... | collective-permute-start | bytes 393224 | tf_op jit(solution)/shard_map/ppermute | solution.py:192
  74.4 11.3 %collective-permute-start.10 = (bf16[64,1024]{1,0:T(8,128)(2,1)S(1)}, bf16[64,1024]{1,0:T(8,128)(2,1)S(1)}, u32[]{:S(2)}, u32[]{:S(2)}) collective-permute-start(bf16[64,1024]{1,0:T(8,128)(2,1)S(1)} %get-tuple-element.36), channel_id=1, source_target_pairs={{0,3},{1,2},{2,1},{3,0},{4,7},{5,6},{6,5},{7,4},{8,11},{9,10},{10,... | collective-permute-start | bytes 393224 | tf_op jit(solution)/shard_map/ppermute | solution.py:192
  79.5 9.6 %collective-permute-start.9 = (bf16[64,1024]{1,0:T(8,128)(2,1)S(1)}, bf16[64,1024]{1,0:T(8,128)(2,1)S(1)}, u32[]{:S(2)}, u32[]{:S(2)}) collective-permute-start(bf16[64,1024]{1,0:T(8,128)(2,1)S(1)} %get-tuple-element.35), channel_id=1, source_target_pairs={{0,2},{1,3},{2,0},{3,1},{4,6},{5,7},{6,4},{7,5},{8,10},{9,11},{10,... | collective-permute-start | bytes 393224 | tf_op jit(solution)/shard_map/ppermute | solution.py:192
  80.2 8.9 %collective-permute-start.6 = (bf16[64,1024]{1,0:T(8,128)(2,1)S(1)}, bf16[64,1024]{1,0:T(8,128)(2,1)S(1)}, u32[]{:S(2)}, u32[]{:S(2)}) collective-permute-start(bf16[64,1024]{1,0:T(8,128)(2,1)S(1)} %get-tuple-element.32), channel_id=1, source_target_pairs={{0,1},{1,0},{2,3},{3,2},{4,5},{5,4},{6,7},{7,6},{8,9},{9,8},{10,11... | collective-permute-start | bytes 393224 | tf_op jit(solution)/shard_map/ppermute | solution.py:192
  (3 other events, 2.3 us)
where the time goes:
time: 91 us; the launch traced here: 90.2 us
  starting transfers between devices  44 us (48%)
  waiting for transfers between devices  23.9 us (26%)
  Pallas kernels  14.6 us (16%)
  local copies, waits for them, and re-layouts  6.46 us (7%)
  other arithmetic  1.1 us (1%)
    ppermute x18, starting transfers between devices, swap(): lax.ppermute(block, 'head', [(i, i ^ distance) for i in range(count)])  40.5 us
    ppermute x18, waiting for transfers between devices, swap(): lax.ppermute(block, 'head', [(i, i ^ distance) for i in range(count)])  23.8 us
    pallas_call x8, Pallas kernels, call(): pl.pallas_call(kernel, out_shape=shapes, in_specs=specs, out_specs=[vmem]...  14.6 us
    unnamed x20, local copies, waits for them, and re-layouts  6.44 us
    ppermute x1, starting transfers between devices, layer(): lax.ppermute(upper, 'blk', [(i, i + 1) for i in range(blocks - 1)])  3.41 us
  transfers between devices with their start and end apart: 19, of which 8 were waited for; matrix products, arithmetic and copies ran while one was open for 3% of the time, Pallas kernels for 15%

commit v1 on v0

--- a/solution.py
+++ b/solution.py
@@ -65,13 +65,40 @@
     out[:, width:] = jnp.where(lane == 0, column, 0.0).astype(jnp.bfloat16)
 
 
-def prepare_kernel(distances, local, scal, queries, exponents, latent, segments, padded, *outs):
-    latent_part(latent, segments, padded)
-    scale_part(distances, local, scal, queries, exponents, outs)
-
-
-def scale_kernel(distances, local, scal, queries, exponents, *outs):
-    scale_part(distances, local, scal, queries, exponents, outs)
+def prepare_kernel(distances, local, scal, queries, exponents, latent, segments, padded, *rest):
+    outs, (queries_here, exponents_here, latent_here, segments_here, sems) = rest[:-5], rest[-5:]
+    copies = [
+        pltpu.make_async_copy(source, target, sems.at[k])
+        for k, (source, target) in enumerate(
+            (
+                (latent, latent_here),
+                (segments, segments_here),
+                (exponents, exponents_here),
+                (queries, queries_here),
+            )
+        )
+    ]
+    for copy in copies:
+        copy.start()
+    copies[0].wait()
+    copies[1].wait()
+    latent_part(latent_here, segments_here, padded)
+    copies[2].wait()
+    copies[3].wait()
+    scale_part(distances, local, scal, queries_here, exponents_here, outs)
+
+
+def scale_kernel(distances, local, scal, queries, exponents, *rest):
+    outs, (queries_here, exponents_here, sems) = rest[:-3], rest[-3:]
+    copies = [
+        pltpu.make_async_copy(exponents, exponents_here, sems.at[0]),
+        pltpu.make_async_copy(queries, queries_here, sems.at[1]),
+    ]
+    for copy in copies:
+        copy.start()
+    for copy in copies:
+        copy.wait()
+    scale_part(distances, local, scal, queries_here, exponents_here, outs)
 
 
 def project_kernel(rows, chips, scal, mine, theirs, key_weight, value_weight, keys, values, tail, window):
@@ -158,10 +185,15 @@
         out[:, pl.ds(pl.multiple_of((scal[0] ^ distance) * width, LANES), width)] = piece[...]
 
 
-def call(kernel, outs, *args, scratch=(), flops=0, nbytes=0, exps=0):
+def call(kernel, outs, *args, scratch=(), flops=0, nbytes=0, exps=0, fetched=False):
     vmem = pl.BlockSpec(memory_space=pltpu.VMEM)
     smem = pl.BlockSpec(memory_space=pltpu.SMEM)
-    specs = [smem] + [vmem] * (len(args) - 1)
+    hbm = pl.BlockSpec(memory_space=pltpu.HBM)
+    specs = [smem] + [hbm if fetched else vmem] * (len(args) - 1)
+    if fetched:
+        scratch = [pltpu.VMEM(arg.shape, arg.dtype) for arg in args[1:]]
+        scratch.append(pltpu.SemaphoreType.DMA((len(args) - 1,)))
+        args = args[:1] + tuple(pltpu.with_memory_space_constraint(arg, pltpu.HBM) for arg in args[1:])
     shapes = [jax.ShapeDtypeStruct(shape, jnp.bfloat16) for shape in outs]
     return pl.pallas_call(
         kernel,
@@ -203,9 +235,16 @@
         latent,
         segments.reshape(1, rows),
         nbytes=2000000,
+        fetched=True,
     )
     near_pieces = call(
-        functools.partial(scale_kernel, near, local), [piece] * len(near), scal, queries, exponents, nbytes=2000000
+        functools.partial(scale_kernel, near, local),
+        [piece] * len(near),
+        scal,
+        queries,
+        exponents,
+        nbytes=2000000,
+        fetched=True,
     )
     sent = list(near_pieces) + list(far_pieces)
 

time: 91 us -> 87.7 us (0.964)
  local copies, waits for them, and re-layouts: 6.46 us -> 0.09 us
  Pallas kernels: 14.6 us -> 17.5 us
  waiting for transfers between devices: 23.9 us -> 25 us
    unnamed x20 -> x8, local copies, waits for them, and re-layouts: 6.44 us -> 0.07 us
    pallas_call x8, Pallas kernels: 14.6 us -> 17.5 us  [call(): pl.pallas_call(kernel, out_shape=shapes, in_specs=specs, out_specs=[vmem]...]
    ppermute x1, waiting for transfers between devices: 0.1 us -> 2.75 us  [layer(): lax.ppermute(upper, 'blk', [(i, i + 1) for i in range(blocks - 1)])]
    ppermute x18, waiting for transfers between devices: 23.8 us -> 22.2 us  [swap(): lax.ppermute(block, 'head', [(i, i ^ distance) for i in range(count)])]
  transfers between devices with their start and end apart: 19 -> 19, of which waited for: 8 -> 8; matrix products, arithmetic and copies ran while one was open for 3% -> 0% of each run, Pallas kernels for 15% -> 17%
where the time goes in v1:
time: 87.7 us; the launch traced here: 87.1 us
  starting transfers between devices  44 us (50%)
  waiting for transfers between devices  25 us (29%)
  Pallas kernels  17.5 us (20%)
    ppermute x18, starting transfers between devices, swap(): lax.ppermute(block, 'head', [(i, i ^ distance) for i in range(count)])  40.6 us
    ppermute x18, waiting for transfers between devices, swap(): lax.ppermute(block, 'head', [(i, i ^ distance) for i in range(count)])  22.2 us
    pallas_call x8, Pallas kernels, call(): pl.pallas_call(kernel, out_shape=shapes, in_specs=specs, out_specs=[vmem]...  17.5 us
    ppermute x1, starting transfers between devices, layer(): lax.ppermute(upper, 'blk', [(i, i + 1) for i in range(blocks - 1)])  3.4 us
    ppermute x1, waiting for transfers between devices, layer(): lax.ppermute(upper, 'blk', [(i, i + 1) for i in range(blocks - 1)])  2.75 us
  transfers between devices with their start and end apart: 19, of which 8 were waited for; matrix products, arithmetic and copies ran while one was open for 0% of the time, Pallas kernels for 17%

profile of v1, /device:TPU:0, one launch (start us, length us, event | category | flops | bytes accessed | tf_op | source)
XLA Modules:
  0.0 87.1 jit_solution(9044731996770782688)
XLA Ops:
  0.0 2.0 %shard_map.65 = (bf16[64,640]{1,0:T(8,128)(2,1)S(1)}, bf16[64,1536]{1,0:T(8,128)(2,1)S(1)}, bf16[64,1536]{1,0:T(8,128)(2,1)S(1)}, bf16[64,1536]{1,0:T(8,128)(2,1)S(1)}, bf16[64,1536]{1,0:T(8,128)(2,1)S(1)}) custom-call(s32[1]{0:T(128)} %bitcast.scal, bf16[64,12288]{1,0:T(8,128)(2,1)} %queries.3, s32[64,64]{1,0:T(8,128)} %exponents.3, ...), custom_call_target="tpu_custom_call" | custom-call | bytes 2000000 | tf_op jit(solution)/shard_map/pallas_call | solution.py:198
  2.0 3.1 %collective-permute-start.1 = (bf16[64,640]{1,0:T(8,128)(2,1)S(1)}, bf16[64,640]{1,0:T(8,128)(2,1)S(1)}, u32[]{:S(2)}, u32[]{:S(2)}) collective-permute-start(bf16[64,640]{1,0:T(8,128)(2,1)S(1)} %get-tuple-element.27), channel_id=1, source_target_pairs={{0,2},{1,3},{2,0},{3,1},{4,6},{5,7},{6,4},{7,5},{8,10},{9,11},{10,... | collective-permute-start | bytes 245768 | tf_op jit(solution)/shard_map/ppermute | solution.py:224
  5.1 2.6 %collective-permute-start.2 = (bf16[64,640]{1,0:T(8,128)(2,1)S(1)}, bf16[64,640]{1,0:T(8,128)(2,1)S(1)}, u32[]{:S(2)}, u32[]{:S(2)}) collective-permute-start(bf16[64,640]{1,0:T(8,128)(2,1)S(1)} %get-tuple-element.27), channel_id=1, source_target_pairs={{0,4},{1,5},{2,6},{3,7},{4,0},{5,1},{6,2},{7,3},{8,12},{9,13},{10,... | collective-permute-start | bytes 245768 | tf_op jit(solution)/shard_map/ppermute | solution.py:224
  7.7 6.6 %collective-permute-done.2 = bf16[64,640]{1,0:T(8,128)(2,1)S(1)} collective-permute-done((bf16[64,640]{1,0:T(8,128)(2,1)S(1)}, bf16[64,640]{1,0:T(8,128)(2,1)S(1)}, u32[]{:S(2)}, u32[]{:S(2)}) %collective-permute-start.2) | collective-permute-done | bytes 81952 | tf_op jit(solution)/shard_map/ppermute | solution.py:224
  14.6 3.4 %collective-permute-start.4 = (bf16[128,640]{1,0:T(8,128)(2,1)S(1)}, bf16[128,640]{1,0:T(8,128)(2,1)S(1)}, u32[]{:S(2)}, u32[]{:S(2)}) collective-permute-start(bf16[128,640]{1,0:T(8,128)(2,1)S(1)} %fusion.2), channel_id=1, source_target_pairs={{0,8},{8,16},{16,24},{1,9},{9,17},{17,25},{2,10},{10,18},{18,26},{... | collective-permute-start | bytes 491528 | tf_op jit(solution)/shard_map/ppermute | solution.py:255
  18.1 2.7 %collective-permute-done.4 = bf16[128,640]{1,0:T(8,128)(2,1)S(1)} collective-permute-done((bf16[128,640]{1,0:T(8,128)(2,1)S(1)}, bf16[128,640]{1,0:T(8,128)(2,1)S(1)}, u32[]{:S(2)}, u32[]{:S(2)}) %collective-permute-start.4) | collective-permute-done | bytes 163872 | tf_op jit(solution)/shard_map/ppermute | solution.py:255
  21.0 2.5 %collective-permute-start.15 = (bf16[64,1536]{1,0:T(8,128)(2,1)S(1)}, bf16[64,1536]{1,0:T(8,128)(2,1)S(1)}, u32[]{:S(2)}, u32[]{:S(2)}) collective-permute-start(bf16[64,1536]{1,0:T(8,128)(2,1)S(1)} %get-tuple-element.41), channel_id=1, source_target_pairs={{0,6},{1,7},{2,4},{3,5},{4,2},{5,3},{6,0},{7,1},{8,14},{9,15},{10,... | collective-permute-start | bytes 589832 | tf_op jit(solution)/shard_map/ppermute | solution.py:224
  25.2 2.0 %collective-permute-start.12 = (bf16[64,1536]{1,0:T(8,128)(2,1)S(1)}, bf16[64,1536]{1,0:T(8,128)(2,1)S(1)}, u32[]{:S(2)}, u32[]{:S(2)}) collective-permute-start(bf16[64,1536]{1,0:T(8,128)(2,1)S(1)} %get-tuple-element.38), channel_id=1, source_target_pairs={{0,5},{1,4},{2,7},{3,6},{4,1},{5,0},{6,3},{7,2},{8,13},{9,12},{10,... | collective-permute-start | bytes 589832 | tf_op jit(solution)/shard_map/ppermute | solution.py:224
  27.2 1.9 %shard_map.64 = (bf16[64,1536]{1,0:T(8,128)(2,1)S(1)}, bf16[64,1536]{1,0:T(8,128)(2,1)S(1)}, bf16[64,1536]{1,0:T(8,128)(2,1)S(1)}, bf16[64,1536]{1,0:T(8,128)(2,1)S(1)}) custom-call(s32[1]{0:T(128)} %bitcast.scal, bf16[64,12288]{1,0:T(8,128)(2,1)} %queries.3, s32[64,64]{1,0:T(8,128)} %exponents.3), custom_call_target="tpu_custom_call" | custom-call | bytes 2000000 | tf_op jit(solution)/shard_map/pallas_call | solution.py:198
  29.1 1.6 %collective-permute-done.15.mine = bf16[64,1536]{1,0:T(8,128)(2,1)S(1)} collective-permute-done((bf16[64,1536]{1,0:T(8,128)(2,1)S(1)}, bf16[64,1536]{1,0:T(8,128)(2,1)S(1)}, u32[]{:S(2)}, u32[]{:S(2)}) %collective-permute-start.15) | collective-permute-done | bytes 196640 | tf_op jit(solution)/shard_map/ppermute | solution.py:224
  30.7 16.4 %collective-permute-start.7 = (bf16[64,1536]{1,0:T(8,128)(2,1)S(1)}, bf16[64,1536]{1,0:T(8,128)(2,1)S(1)}, u32[]{:S(2)}, u32[]{:S(2)}) collective-permute-start(bf16[64,1536]{1,0:T(8,128)(2,1)S(1)} %get-tuple-element.33), channel_id=1, source_target_pairs={{0,2},{1,3},{2,0},{3,1},{4,6},{5,7},{6,4},{7,5},{8,10},{9,11},{10,... | collective-permute-start | bytes 589832 | tf_op jit(solution)/shard_map/ppermute | solution.py:224
  47.1 3.9 %collective-permute-start.8 = (bf16[64,1536]{1,0:T(8,128)(2,1)S(1)}, bf16[64,1536]{1,0:T(8,128)(2,1)S(1)}, u32[]{:S(2)}, u32[]{:S(2)}) collective-permute-start(bf16[64,1536]{1,0:T(8,128)(2,1)S(1)} %get-tuple-element.34), channel_id=1, source_target_pairs={{0,3},{1,2},{2,1},{3,0},{4,7},{5,6},{6,5},{7,4},{8,11},{9,10},{10,... | collective-permute-start | bytes 589832 | tf_op jit(solution)/shard_map/ppermute | solution.py:224
  51.0 2.5 %shard_map.66 = (bf16[768,1024]{1,0:T(8,128)(2,1)S(1)}, bf16[768,1024]{1,0:T(8,128)(2,1)S(1)}, bf16[768,128]{1,0:T(8,128)(2,1)S(1)}) custom-call(s32[1]{0:T(128)} %bitcast.scal, bf16[384,640]{1,0:T(8,128)(2,1)S(1)} %constant_dynamic-update-slice_fusion.mine, bf16[384,640]{1,0:T(8,128)(2,1)S(1)} %collective-permute-done.5.theirs, ...), custom_call_target="tpu_custom_call" | custom-call | flops 1610612736 | bytes 2097152 | tf_op jit(solution)/shard_map/pallas_call | solution.py:198
  53.6 2.5 %shard_map.70 = (bf16[64,1024]{1,0:T(8,128)(2,1)S(1)}, bf16[64,1024]{1,0:T(8,128)(2,1)S(1)}) custom-call(s32[1]{0:T(128)} %bitcast.scal, bf16[64,1536]{1,0:T(8,128)(2,1)S(1)} %collective-permute-done.15.mine, bf16[64,1536]{1,0:T(8,128)(2,1)S(1)} %collective-permute-done.16.theirs, bf16[768,1024]{1,0:T(8,128)(2,1)S(1)} %get-tuple-element.28.keys, ...), custom_call_target="tpu_custom_call" | custom-call | flops 301989888 | bytes 655360 | tf_op jit(solution)/shard_map/pallas_call | solution.py:198
  56.1 2.5 %collective-permute-start.17 = (bf16[64,1024]{1,0:T(8,128)(2,1)S(1)}, bf16[64,1024]{1,0:T(8,128)(2,1)S(1)}, u32[]{:S(2)}, u32[]{:S(2)}) collective-permute-start(bf16[64,1024]{1,0:T(8,128)(2,1)S(1)} %get-tuple-element.43), channel_id=1, source_target_pairs={{0,6},{1,7},{2,4},{3,5},{4,2},{5,3},{6,0},{7,1},{8,14},{9,15},{10,... | collective-permute-start | bytes 393224 | tf_op jit(solution)/shard_map/ppermute | solution.py:224
  58.7 2.0 %collective-permute-start.18 = (bf16[64,1024]{1,0:T(8,128)(2,1)S(1)}, bf16[64,1024]{1,0:T(8,128)(2,1)S(1)}, u32[]{:S(2)}, u32[]{:S(2)}) collective-permute-start(bf16[64,1024]{1,0:T(8,128)(2,1)S(1)} %get-tuple-element.44), channel_id=1, source_target_pairs={{0,7},{1,6},{2,5},{3,4},{4,3},{5,2},{6,1},{7,0},{8,15},{9,14},{10,... | collective-permute-start | bytes 393224 | tf_op jit(solution)/shard_map/ppermute | solution.py:224
  60.6 2.5 %shard_map.69 = (bf16[64,1024]{1,0:T(8,128)(2,1)S(1)}, bf16[64,1024]{1,0:T(8,128)(2,1)S(1)}) custom-call(s32[1]{0:T(128)} %bitcast.scal, bf16[64,1536]{1,0:T(8,128)(2,1)S(1)} %collective-permute-done.11.mine, bf16[64,1536]{1,0:T(8,128)(2,1)S(1)} %collective-permute-done.12.theirs, bf16[768,1024]{1,0:T(8,128)(2,1)S(1)} %get-tuple-element.28.keys, ...), custom_call_target="tpu_custom_call" | custom-call | flops 301989888 | bytes 655360 | tf_op jit(solution)/shard_map/pallas_call | solution.py:198
  63.3 5.3 %collective-permute-done.8.theirs = bf16[64,1536]{1,0:T(8,128)(2,1)S(1)} collective-permute-done((bf16[64,1536]{1,0:T(8,128)(2,1)S(1)}, bf16[64,1536]{1,0:T(8,128)(2,1)S(1)}, u32[]{:S(2)}, u32[]{:S(2)}) %collective-permute-start.8) | collective-permute-done | bytes 196640 | tf_op jit(solution)/shard_map/ppermute | solution.py:224
  68.8 2.5 %shard_map.68 = (bf16[64,1024]{1,0:T(8,128)(2,1)S(1)}, bf16[64,1024]{1,0:T(8,128)(2,1)S(1)}) custom-call(s32[1]{0:T(128)} %bitcast.scal, bf16[64,1536]{1,0:T(8,128)(2,1)S(1)} %collective-permute-done.7.mine, bf16[64,1536]{1,0:T(8,128)(2,1)S(1)} %collective-permute-done.8.theirs, bf16[768,1024]{1,0:T(8,128)(2,1)S(1)} %get-tuple-element.28.keys, ...), custom_call_target="tpu_custom_call" | custom-call | flops 301989888 | bytes 655360 | tf_op jit(solution)/shard_map/pallas_call | solution.py:198
  71.4 2.6 %collective-permute-start.10 = (bf16[64,1024]{1,0:T(8,128)(2,1)S(1)}, bf16[64,1024]{1,0:T(8,128)(2,1)S(1)}, u32[]{:S(2)}, u32[]{:S(2)}) collective-permute-start(bf16[64,1024]{1,0:T(8,128)(2,1)S(1)} %get-tuple-element.36), channel_id=1, source_target_pairs={{0,3},{1,2},{2,1},{3,0},{4,7},{5,6},{6,5},{7,4},{8,11},{9,10},{10,... | collective-permute-start | bytes 393224 | tf_op jit(solution)/shard_map/ppermute | solution.py:224
  73.9 2.5 %shard_map.67 = (bf16[64,1024]{1,0:T(8,128)(2,1)S(1)}, bf16[64,1024]{1,0:T(8,128)(2,1)S(1)}) custom-call(s32[1]{0:T(128)} %bitcast.scal, bf16[64,1536]{1,0:T(8,128)(2,1)S(1)} %get-tuple-element.25.mine, bf16[64,1536]{1,0:T(8,128)(2,1)S(1)} %collective-permute-done.theirs, bf16[768,1024]{1,0:T(8,128)(2,1)S(1)} %get-tuple-element.28.keys, ...), custom_call_target="tpu_custom_call" | custom-call | flops 301989888 | bytes 655360 | tf_op jit(solution)/shard_map/pallas_call | solution.py:198
  77.3 1.8 %collective-permute-done.13.refs_4_ = bf16[64,1024]{1,0:T(8,128)(2,1)S(1)} collective-permute-done((bf16[64,1024]{1,0:T(8,128)(2,1)S(1)}, bf16[64,1024]{1,0:T(8,128)(2,1)S(1)}, u32[]{:S(2)}, u32[]{:S(2)}) %collective-permute-start.13) | collective-permute-done | bytes 131104 | tf_op jit(solution)/shard_map/ppermute | solution.py:224
  80.5 2.1 %collective-permute-done.10.refs_3_ = bf16[64,1024]{1,0:T(8,128)(2,1)S(1)} collective-permute-done((bf16[64,1024]{1,0:T(8,128)(2,1)S(1)}, bf16[64,1024]{1,0:T(8,128)(2,1)S(1)}, u32[]{:S(2)}, u32[]{:S(2)}) %collective-permute-start.10) | collective-permute-done | bytes 131104 | tf_op jit(solution)/shard_map/ppermute | solution.py:224
  82.7 3.4 %collective-permute-done.9.refs_2_ = bf16[64,1024]{1,0:T(8,128)(2,1)S(1)} collective-permute-done((bf16[64,1024]{1,0:T(8,128)(2,1)S(1)}, bf16[64,1024]{1,0:T(8,128)(2,1)S(1)}, u32[]{:S(2)}, u32[]{:S(2)}) %collective-permute-start.9) | collective-permute-done | bytes 131104 | tf_op jit(solution)/shard_map/ppermute | solution.py:224
  (32 shorter events, 5.9 us)
Async XLA Ops:
  2.0 49.0 %copy-start = (bf16[512,1024]{1,0:T(8,128)(2,1)S(1)}, bf16[512,1024]{1,0:T(8,128)(2,1)}, u32[]{:S(2)}) copy-start(bf16[512,1024]{1,0:T(8,128)(2,1)} %key_weight.1) | copy-start | bytes 3145732
  2.0 49.0 %copy-start.1 = (bf16[512,1024]{1,0:T(8,128)(2,1)S(1)}, bf16[512,1024]{1,0:T(8,128)(2,1)}, u32[]{:S(2)}) copy-start(bf16[512,1024]{1,0:T(8,128)(2,1)} %value_weight.1) | copy-start | bytes 3145732
  2.0 5.7 %collective-permute-start.1 = (bf16[64,640]{1,0:T(8,128)(2,1)S(1)}, bf16[64,640]{1,0:T(8,128)(2,1)S(1)}, u32[]{:S(2)}, u32[]{:S(2)}) collective-permute-start(bf16[64,640]{1,0:T(8,128)(2,1)S(1)} %get-tuple-element.27), channel_id=1, source_target_pairs={{0,2},{1,3},{2,0},{3,1},{4,6},{5,7},{6,4},{7,5},{8,10},{9,11},{10,... | collective-permute-start | bytes 245768 | tf_op jit(solution)/shard_map/ppermute | solution.py:224
  5.1 9.2 %collective-permute-start.2 = (bf16[64,640]{1,0:T(8,128)(2,1)S(1)}, bf16[64,640]{1,0:T(8,128)(2,1)S(1)}, u32[]{:S(2)}, u32[]{:S(2)}) collective-permute-start(bf16[64,640]{1,0:T(8,128)(2,1)S(1)} %get-tuple-element.27), channel_id=1, source_target_pairs={{0,4},{1,5},{2,6},{3,7},{4,0},{5,1},{6,2},{7,3},{8,12},{9,13},{10,... | collective-permute-start | bytes 245768 | tf_op jit(solution)/shard_map/ppermute | solution.py:224
  7.7 6.6 %collective-permute-start.3 = (bf16[64,640]{1,0:T(8,128)(2,1)S(1)}, bf16[64,640]{1,0:T(8,128)(2,1)S(1)}, u32[]{:S(2)}, u32[]{:S(2)}) collective-permute-start(bf16[64,640]{1,0:T(8,128)(2,1)S(1)} %get-tuple-element.27), channel_id=1, source_target_pairs={{0,6},{1,7},{2,4},{3,5},{4,2},{5,3},{6,0},{7,1},{8,14},{9,15},{10,... | collective-permute-start | bytes 245768 | tf_op jit(solution)/shard_map/ppermute | solution.py:224
  14.6 6.2 %collective-permute-start.4 = (bf16[128,640]{1,0:T(8,128)(2,1)S(1)}, bf16[128,640]{1,0:T(8,128)(2,1)S(1)}, u32[]{:S(2)}, u32[]{:S(2)}) collective-permute-start(bf16[128,640]{1,0:T(8,128)(2,1)S(1)} %fusion.2), channel_id=1, source_target_pairs={{0,8},{8,16},{16,24},{1,9},{9,17},{17,25},{2,10},{10,18},{18,26},{... | collective-permute-start | bytes 491528 | tf_op jit(solution)/shard_map/ppermute | solution.py:255
  20.9 30.1 %collective-permute-start.5 = (bf16[384,640]{1,0:T(8,128)(2,1)S(1)}, bf16[384,640]{1,0:T(8,128)(2,1)S(1)}, u32[]{:S(2)}, u32[]{:S(2)}) collective-permute-start(bf16[384,640]{1,0:T(8,128)(2,1)S(1)} %constant_dynamic-update-slice_fusion.mine), channel_id=1, source_target_pairs={{0,1},{1,0},{2,3},{3,2},{4,5},{5,4},{6,7},{7,6},{8,9},{9,8},{10,11... | collective-permute-start | bytes 1474568 | tf_op jit(solution)/shard_map/ppermute | solution.py:224
  21.0 9.7 %collective-permute-start.15 = (bf16[64,1536]{1,0:T(8,128)(2,1)S(1)}, bf16[64,1536]{1,0:T(8,128)(2,1)S(1)}, u32[]{:S(2)}, u32[]{:S(2)}) collective-permute-start(bf16[64,1536]{1,0:T(8,128)(2,1)S(1)} %get-tuple-element.41), channel_id=1, source_target_pairs={{0,6},{1,7},{2,4},{3,5},{4,2},{5,3},{6,0},{7,1},{8,14},{9,15},{10,... | collective-permute-start | bytes 589832 | tf_op jit(solution)/shard_map/ppermute | solution.py:224
  23.5 23.6 %collective-permute-start.16 = (bf16[64,1536]{1,0:T(8,128)(2,1)S(1)}, bf16[64,1536]{1,0:T(8,128)(2,1)S(1)}, u32[]{:S(2)}, u32[]{:S(2)}) collective-permute-start(bf16[64,1536]{1,0:T(8,128)(2,1)S(1)} %get-tuple-element.42), channel_id=1, source_target_pairs={{0,7},{1,6},{2,5},{3,4},{4,3},{5,2},{6,1},{7,0},{8,15},{9,14},{10,... | collective-permute-start | bytes 589832 | tf_op jit(solution)/shard_map/ppermute | solution.py:224
  24.6 31.5 %collective-permute-start.11 = (bf16[64,1536]{1,0:T(8,128)(2,1)S(1)}, bf16[64,1536]{1,0:T(8,128)(2,1)S(1)}, u32[]{:S(2)}, u32[]{:S(2)}) collective-permute-start(bf16[64,1536]{1,0:T(8,128)(2,1)S(1)} %get-tuple-element.37), channel_id=1, source_target_pairs={{0,4},{1,5},{2,6},{3,7},{4,0},{5,1},{6,2},{7,3},{8,12},{9,13},{10,... | collective-permute-start | bytes 589832 | tf_op jit(solution)/shard_map/ppermute | solution.py:224
  25.2 33.4 %collective-permute-start.12 = (bf16[64,1536]{1,0:T(8,128)(2,1)S(1)}, bf16[64,1536]{1,0:T(8,128)(2,1)S(1)}, u32[]{:S(2)}, u32[]{:S(2)}) collective-permute-start(bf16[64,1536]{1,0:T(8,128)(2,1)S(1)} %get-tuple-element.38), channel_id=1, source_target_pairs={{0,5},{1,4},{2,7},{3,6},{4,1},{5,0},{6,3},{7,2},{8,13},{9,12},{10,... | collective-permute-start | bytes 589832 | tf_op jit(solution)/shard_map/ppermute | solution.py:224
  30.7 32.5 %collective-permute-start.7 = (bf16[64,1536]{1,0:T(8,128)(2,1)S(1)}, bf16[64,1536]{1,0:T(8,128)(2,1)S(1)}, u32[]{:S(2)}, u32[]{:S(2)}) collective-permute-start(bf16[64,1536]{1,0:T(8,128)(2,1)S(1)} %get-tuple-element.33), channel_id=1, source_target_pairs={{0,2},{1,3},{2,0},{3,1},{4,6},{5,7},{6,4},{7,5},{8,10},{9,11},{10,... | collective-permute-start | bytes 589832 | tf_op jit(solution)/shard_map/ppermute | solution.py:224
  47.1 21.5 %collective-permute-start.8 = (bf16[64,1536]{1,0:T(8,128)(2,1)S(1)}, bf16[64,1536]{1,0:T(8,128)(2,1)S(1)}, u32[]{:S(2)}, u32[]{:S(2)}) collective-permute-start(bf16[64,1536]{1,0:T(8,128)(2,1)S(1)} %get-tuple-element.34), channel_id=1, source_target_pairs={{0,3},{1,2},{2,1},{3,0},{4,7},{5,6},{6,5},{7,4},{8,11},{9,10},{10,... | collective-permute-start | bytes 589832 | tf_op jit(solution)/shard_map/ppermute | solution.py:224
  51.0 20.3 %collective-permute-start = (bf16[64,1536]{1,0:T(8,128)(2,1)S(1)}, bf16[64,1536]{1,0:T(8,128)(2,1)S(1)}, u32[]{:S(2)}, u32[]{:S(2)}) collective-permute-start(bf16[64,1536]{1,0:T(8,128)(2,1)S(1)} %get-tuple-element.26), channel_id=1, source_target_pairs={{0,1},{1,0},{2,3},{3,2},{4,5},{5,4},{6,7},{7,6},{8,9},{9,8},{10,11... | collective-permute-start | bytes 589832 | tf_op jit(solution)/shard_map/ppermute | solution.py:224
  56.1 20.3 %collective-permute-start.17 = (bf16[64,1024]{1,0:T(8,128)(2,1)S(1)}, bf16[64,1024]{1,0:T(8,128)(2,1)S(1)}, u32[]{:S(2)}, u32[]{:S(2)}) collective-permute-start(bf16[64,1024]{1,0:T(8,128)(2,1)S(1)} %get-tuple-element.43), channel_id=1, source_target_pairs={{0,6},{1,7},{2,4},{3,5},{4,2},{5,3},{6,0},{7,1},{8,14},{9,15},{10,... | collective-permute-start | bytes 393224 | tf_op jit(solution)/shard_map/ppermute | solution.py:224
  58.7 18.5 %collective-permute-start.18 = (bf16[64,1024]{1,0:T(8,128)(2,1)S(1)}, bf16[64,1024]{1,0:T(8,128)(2,1)S(1)}, u32[]{:S(2)}, u32[]{:S(2)}) collective-permute-start(bf16[64,1024]{1,0:T(8,128)(2,1)S(1)} %get-tuple-element.44), channel_id=1, source_target_pairs={{0,7},{1,6},{2,5},{3,4},{4,3},{5,2},{6,1},{7,0},{8,15},{9,14},{10,... | collective-permute-start | bytes 393224 | tf_op jit(solution)/shard_map/ppermute | solution.py:224
  63.2 16.0 %collective-permute-start.13 = (bf16[64,1024]{1,0:T(8,128)(2,1)S(1)}, bf16[64,1024]{1,0:T(8,128)(2,1)S(1)}, u32[]{:S(2)}, u32[]{:S(2)}) collective-permute-start(bf16[64,1024]{1,0:T(8,128)(2,1)S(1)} %get-tuple-element.39), channel_id=1, source_target_pairs={{0,4},{1,5},{2,6},{3,7},{4,0},{5,1},{6,2},{7,3},{8,12},{9,13},{10,... | collective-permute-start | bytes 393224 | tf_op jit(solution)/shard_map/ppermute | solution.py:224
  68.5 12.0 %collective-permute-start.14 = (bf16[64,1024]{1,0:T(8,128)(2,1)S(1)}, bf16[64,1024]{1,0:T(8,128)(2,1)S(1)}, u32[]{:S(2)}, u32[]{:S(2)}) collective-permute-start(bf16[64,1024]{1,0:T(8,128)(2,1)S(1)} %get-tuple-element.40), channel_id=1, source_target_pairs={{0,5},{1,4},{2,7},{3,6},{4,1},{5,0},{6,3},{7,2},{8,13},{9,12},{10,... | collective-permute-start | bytes 393224 | tf_op jit(solution)/shard_map/ppermute | solution.py:224
  71.4 11.3 %collective-permute-start.10 = (bf16[64,1024]{1,0:T(8,128)(2,1)S(1)}, bf16[64,1024]{1,0:T(8,128)(2,1)S(1)}, u32[]{:S(2)}, u32[]{:S(2)}) collective-permute-start(bf16[64,1024]{1,0:T(8,128)(2,1)S(1)} %get-tuple-element.36), channel_id=1, source_target_pairs={{0,3},{1,2},{2,1},{3,0},{4,7},{5,6},{6,5},{7,4},{8,11},{9,10},{10,... | collective-permute-start | bytes 393224 | tf_op jit(solution)/shard_map/ppermute | solution.py:224
  76.5 9.6 %collective-permute-start.9 = (bf16[64,1024]{1,0:T(8,128)(2,1)S(1)}, bf16[64,1024]{1,0:T(8,128)(2,1)S(1)}, u32[]{:S(2)}, u32[]{:S(2)}) collective-permute-start(bf16[64,1024]{1,0:T(8,128)(2,1)S(1)} %get-tuple-element.35), channel_id=1, source_target_pairs={{0,2},{1,3},{2,0},{3,1},{4,6},{5,7},{6,4},{7,5},{8,10},{9,11},{10,... | collective-permute-start | bytes 393224 | tf_op jit(solution)/shard_map/ppermute | solution.py:224
  77.2 8.9 %collective-permute-start.6 = (bf16[64,1024]{1,0:T(8,128)(2,1)S(1)}, bf16[64,1024]{1,0:T(8,128)(2,1)S(1)}, u32[]{:S(2)}, u32[]{:S(2)}) collective-permute-start(bf16[64,1024]{1,0:T(8,128)(2,1)S(1)} %get-tuple-element.32), channel_id=1, source_target_pairs={{0,1},{1,0},{2,3},{3,2},{4,5},{5,4},{6,7},{7,6},{8,9},{9,8},{10,11... | collective-permute-start | bytes 393224 | tf_op jit(solution)/shard_map/ppermute | solution.py:224

commit v2 on v1

--- a/solution.py
+++ b/solution.py
@@ -101,18 +101,31 @@
     scale_part(distances, local, scal, queries_here, exponents_here, outs)
 
 
-def project_kernel(rows, chips, scal, mine, theirs, key_weight, value_weight, keys, values, tail, window):
+def pack_kernel(rows, chips, scal, *refs):
+    pieces, (own, upper) = refs[:-2], refs[-2:]
+    for slot, piece in enumerate(pieces):
+        own[slot * rows : (slot + 1) * rows, :] = piece[...]
+    half = chips // 2
+    first = jnp.where(scal[0] // 2 < half, half, 0) * rows
+    upper[...] = own[pl.ds(pl.multiple_of(first, rows), half * rows), :]
+
+
+def project_kernel(
+    rows, chips, scal, own, earlier, other_own, other_earlier, key_weight, value_weight, keys, values, tail, window
+):
     place, core = scal[0] // 2, scal[0] % 2
     lead = chips * rows
-    other_half = jnp.where(place < chips // 2, chips // 2, 0)
-    for slot in range(chips + chips // 2):
+    half = chips // 2
+    first = jnp.where(place < half, half, 0)
+    for slot in range(chips + half):
         if slot < chips:
             to = lead + (place ^ slot) * 2 * rows
+            mine, theirs, at = own, other_own, slot * rows
         else:
-            to = ((place ^ (other_half + slot - chips)) - chips // 2) * 2 * rows
-        take = slice(slot * rows, (slot + 1) * rows)
-        window[pl.ds(pl.multiple_of(to + core * rows, rows), rows), :] = mine[take, :]
-        window[pl.ds(pl.multiple_of(to + (1 - core) * rows, rows), rows), :] = theirs[take, :]
+            to = ((place ^ (first + slot - chips)) - half) * 2 * rows
+            mine, theirs, at = earlier, other_earlier, (slot - chips) * rows
+        window[pl.ds(pl.multiple_of(to + core * rows, rows), rows), :] = mine[at : at + rows, :]
+        window[pl.ds(pl.multiple_of(to + (1 - core) * rows, rows), rows), :] = theirs[at : at + rows, :]
     tail[...] = window[:, LATENT:]
     columns = keys.shape[1]
     tile = min(256, columns)
@@ -185,7 +198,11 @@
         out[:, pl.ds(pl.multiple_of((scal[0] ^ distance) * width, LANES), width)] = piece[...]
 
 
-def call(kernel, outs, *args, scratch=(), flops=0, nbytes=0, exps=0, fetched=False):
+def call(kernel, outs, *args, **options):
+    return kernel_call(kernel, outs, *args, **options)
+
+
+def kernel_call(kernel, outs, *args, scratch=(), flops=0, nbytes=0, exps=0, fetched=False):
     vmem = pl.BlockSpec(memory_space=pltpu.VMEM)
     smem = pl.BlockSpec(memory_space=pltpu.SMEM)
     hbm = pl.BlockSpec(memory_space=pltpu.HBM)
@@ -248,13 +265,25 @@
     )
     sent = list(near_pieces) + list(far_pieces)
 
-    own = [padded] + [swap(padded, 2 * k) for k in range(1, chips)]
-    own = jnp.concatenate(own, axis=0)
-    other_half = jnp.where(position // 2 < chips // 2, chips // 2, 0)
-    upper = lax.dynamic_slice_in_dim(own, other_half * rows, chips // 2 * rows, 0)
+    half = chips // 2
+    pieces = [None] * chips
+    pieces[0] = padded
+    pieces[half] = swap(padded, chips)
+    for k in range(1, half):
+        pieces[k] = swap(padded, 2 * k)
+    for k in range(1, half):
+        pieces[half + k] = swap(pieces[half], 2 * k)
+    row_width = LATENT + 2 * ROPE
+    own, upper = call(
+        functools.partial(pack_kernel, rows, chips),
+        [(lead, row_width), (half * rows, row_width)],
+        scal,
+        *pieces,
+        nbytes=400000,
+    )
+    other_own = swap(own, 1)
     earlier = lax.ppermute(upper, "blk", [(i, i + 1) for i in range(blocks - 1)])
-    mine = jnp.concatenate([own, earlier], axis=0)
-    theirs = swap(mine, 1)
+    other_earlier = swap(earlier, 1)
 
     arrived = [sent[0]] + [swap(sent[distance], distance) for distance in range(1, count)]
 
@@ -262,8 +291,10 @@
         functools.partial(project_kernel, rows, chips),
         [(window_rows, columns), (window_rows, columns), (window_rows, LANES)],
         scal,
-        mine,
-        theirs,
+        own,
+        earlier,
+        other_own,
+        other_earlier,
         key_weight,
         value_weight,
         scratch=[pltpu.VMEM((window_rows, LATENT + LANES), jnp.bfloat16)],

time: 87.7 us -> 86.9 us (level)
  starting transfers between devices: 44 us -> 41.6 us
  waiting for transfers between devices: 25 us -> 27.3 us
    ppermute x18 -> x19, waiting for transfers between devices: 22.2 us -> 27.3 us  [swap(): lax.ppermute(block, 'head', [(i, i ^ distance) for i in range(count)])]
    ppermute x18 -> x19, starting transfers between devices: 40.6 us -> 37.8 us  [swap(): lax.ppermute(block, 'head', [(i, i ^ distance) for i in range(count)])]
    ppermute x1, waiting for transfers between devices: 2.75 us -> 0.01 us  [layer(): lax.ppermute(upper, 'blk', [(i, i + 1) for i in range(blocks - 1)])]
    pallas_call x8 -> x9, Pallas kernels: 17.5 us -> 17.7 us  [kernel_call(): pl.pallas_call(kernel, out_shape=shapes, in_specs=specs, out_specs=[vmem]...]
  transfers between devices with their start and end apart: 19 -> 20, of which waited for: 8 -> 8; matrix products, arithmetic and copies ran while one was open for 0% -> 0% of each run, Pallas kernels for 17% -> 17%
where the time goes in v2:
time: 86.9 us; the launch traced here: 86.7 us
  starting transfers between devices  41.6 us (48%)
  waiting for transfers between devices  27.3 us (31%)
  Pallas kernels  17.7 us (20%)
    ppermute x19, starting transfers between devices, swap(): lax.ppermute(block, 'head', [(i, i ^ distance) for i in range(count)])  37.8 us
    ppermute x19, waiting for transfers between devices, swap(): lax.ppermute(block, 'head', [(i, i ^ distance) for i in range(count)])  27.3 us
    pallas_call x9, Pallas kernels, kernel_call(): pl.pallas_call(kernel, out_shape=shapes, in_specs=specs, out_specs=[vmem]...  17.7 us
    ppermute x1, starting transfers between devices, layer(): lax.ppermute(upper, 'blk', [(i, i + 1) for i in range(blocks - 1)])  3.78 us
  transfers between devices with their start and end apart: 20, of which 8 were waited for; matrix products, arithmetic and copies ran while one was open for 0% of the time, Pallas kernels for 17%

profile of v2, /device:TPU:0, one launch (start us, length us, event | category | flops | bytes accessed | tf_op | source)
XLA Modules:
  0.0 86.7 jit_solution(4649371500299708828)
XLA Ops:
  0.0 2.1 %shard_map.65 = (bf16[64,640]{1,0:T(8,128)(2,1)S(1)}, bf16[64,1536]{1,0:T(8,128)(2,1)S(1)}, bf16[64,1536]{1,0:T(8,128)(2,1)S(1)}, bf16[64,1536]{1,0:T(8,128)(2,1)S(1)}, bf16[64,1536]{1,0:T(8,128)(2,1)S(1)}) custom-call(s32[1]{0:T(128)} %bitcast.scal, bf16[64,12288]{1,0:T(8,128)(2,1)} %queries.3, s32[64,64]{1,0:T(8,128)} %exponents.3, ...), custom_call_target="tpu_custom_call" | custom-call | bytes 2000000 | tf_op jit(solution)/shard_map/pallas_call | solution.py:215
  2.1 4.1 %collective-permute-start.2 = (bf16[64,640]{1,0:T(8,128)(2,1)S(1)}, bf16[64,640]{1,0:T(8,128)(2,1)S(1)}, u32[]{:S(2)}, u32[]{:S(2)}) collective-permute-start(bf16[64,640]{1,0:T(8,128)(2,1)S(1)} %get-tuple-element.29.refs_0_), channel_id=1, source_target_pairs={{0,4},{1,5},{2,6},{3,7},{4,0},{5,1},{6,2},{7,3},{8,12},{9,13},{10,... | collective-permute-start | bytes 245768 | tf_op jit(solution)/shard_map/ppermute | solution.py:241
  6.2 1.6 %collective-permute-start.1 = (bf16[64,640]{1,0:T(8,128)(2,1)S(1)}, bf16[64,640]{1,0:T(8,128)(2,1)S(1)}, u32[]{:S(2)}, u32[]{:S(2)}) collective-permute-start(bf16[64,640]{1,0:T(8,128)(2,1)S(1)} %get-tuple-element.29.refs_0_), channel_id=1, source_target_pairs={{0,2},{1,3},{2,0},{3,1},{4,6},{5,7},{6,4},{7,5},{8,10},{9,11},{10,... | collective-permute-start | bytes 245768 | tf_op jit(solution)/shard_map/ppermute | solution.py:241
  7.8 2.2 %collective-permute-done.2.refs_2_ = bf16[64,640]{1,0:T(8,128)(2,1)S(1)} collective-permute-done((bf16[64,640]{1,0:T(8,128)(2,1)S(1)}, bf16[64,640]{1,0:T(8,128)(2,1)S(1)}, u32[]{:S(2)}, u32[]{:S(2)}) %collective-permute-start.2) | collective-permute-done | bytes 81952 | tf_op jit(solution)/shard_map/ppermute | solution.py:241
  11.2 3.2 %collective-permute-done.3.refs_3_ = bf16[64,640]{1,0:T(8,128)(2,1)S(1)} collective-permute-done((bf16[64,640]{1,0:T(8,128)(2,1)S(1)}, bf16[64,640]{1,0:T(8,128)(2,1)S(1)}, u32[]{:S(2)}, u32[]{:S(2)}) %collective-permute-start.3) | collective-permute-done | bytes 81952 | tf_op jit(solution)/shard_map/ppermute | solution.py:241
  14.5 3.8 %collective-permute-start.4 = (bf16[128,640]{1,0:T(8,128)(2,1)S(1)}, bf16[128,640]{1,0:T(8,128)(2,1)S(1)}, u32[]{:S(2)}, u32[]{:S(2)}) collective-permute-start(bf16[128,640]{1,0:T(8,128)(2,1)S(1)} %get-tuple-element.31), channel_id=1, source_target_pairs={{0,8},{8,16},{16,24},{1,9},{9,17},{17,25},{2,10},{10,18},{18,26},{... | collective-permute-start | bytes 491528 | tf_op jit(solution)/shard_map/ppermute | solution.py:285
  18.4 3.7 %collective-permute-start.16 = (bf16[64,1536]{1,0:T(8,128)(2,1)S(1)}, bf16[64,1536]{1,0:T(8,128)(2,1)S(1)}, u32[]{:S(2)}, u32[]{:S(2)}) collective-permute-start(bf16[64,1536]{1,0:T(8,128)(2,1)S(1)} %get-tuple-element.45), channel_id=1, source_target_pairs={{0,6},{1,7},{2,4},{3,5},{4,2},{5,3},{6,0},{7,1},{8,14},{9,15},{10,... | collective-permute-start | bytes 589832 | tf_op jit(solution)/shard_map/ppermute | solution.py:241
  23.4 4.7 %collective-permute-done.16.mine = bf16[64,1536]{1,0:T(8,128)(2,1)S(1)} collective-permute-done((bf16[64,1536]{1,0:T(8,128)(2,1)S(1)}, bf16[64,1536]{1,0:T(8,128)(2,1)S(1)}, u32[]{:S(2)}, u32[]{:S(2)}) %collective-permute-start.16) | collective-permute-done | bytes 196640 | tf_op jit(solution)/shard_map/ppermute | solution.py:241
  28.1 11.6 %collective-permute-start.13 = (bf16[64,1536]{1,0:T(8,128)(2,1)S(1)}, bf16[64,1536]{1,0:T(8,128)(2,1)S(1)}, u32[]{:S(2)}, u32[]{:S(2)}) collective-permute-start(bf16[64,1536]{1,0:T(8,128)(2,1)S(1)} %get-tuple-element.42), channel_id=1, source_target_pairs={{0,5},{1,4},{2,7},{3,6},{4,1},{5,0},{6,3},{7,2},{8,13},{9,12},{10,... | collective-permute-start | bytes 589832 | tf_op jit(solution)/shard_map/ppermute | solution.py:241
  39.7 1.9 %shard_map.64 = (bf16[64,1536]{1,0:T(8,128)(2,1)S(1)}, bf16[64,1536]{1,0:T(8,128)(2,1)S(1)}, bf16[64,1536]{1,0:T(8,128)(2,1)S(1)}, bf16[64,1536]{1,0:T(8,128)(2,1)S(1)}) custom-call(s32[1]{0:T(128)} %bitcast.scal, bf16[64,12288]{1,0:T(8,128)(2,1)} %queries.3, s32[64,64]{1,0:T(8,128)} %exponents.3), custom_call_target="tpu_custom_call" | custom-call | bytes 2000000 | tf_op jit(solution)/shard_map/pallas_call | solution.py:215
  41.6 6.0 %collective-permute-start.8 = (bf16[64,1536]{1,0:T(8,128)(2,1)S(1)}, bf16[64,1536]{1,0:T(8,128)(2,1)S(1)}, u32[]{:S(2)}, u32[]{:S(2)}) collective-permute-start(bf16[64,1536]{1,0:T(8,128)(2,1)S(1)} %get-tuple-element.37), channel_id=1, source_target_pairs={{0,2},{1,3},{2,0},{3,1},{4,6},{5,7},{6,4},{7,5},{8,10},{9,11},{10,... | collective-permute-start | bytes 589832 | tf_op jit(solution)/shard_map/ppermute | solution.py:241
  47.7 2.5 %shard_map.67 = (bf16[768,1024]{1,0:T(8,128)(2,1)S(1)}, bf16[768,1024]{1,0:T(8,128)(2,1)S(1)}, bf16[768,128]{1,0:T(8,128)(2,1)S(1)}) custom-call(s32[1]{0:T(128)} %bitcast.scal, bf16[256,640]{1,0:T(8,128)(2,1)S(1)} %get-tuple-element.30.own, bf16[128,640]{1,0:T(8,128)(2,1)S(1)} %collective-permute-done.4.earlier, ...), custom_call_target="tpu_custom_call" | custom-call | flops 1610612736 | bytes 2097152 | tf_op jit(solution)/shard_map/pallas_call | solution.py:215
  50.2 2.5 %shard_map.71 = (bf16[64,1024]{1,0:T(8,128)(2,1)S(1)}, bf16[64,1024]{1,0:T(8,128)(2,1)S(1)}) custom-call(s32[1]{0:T(128)} %bitcast.scal, bf16[64,1536]{1,0:T(8,128)(2,1)S(1)} %collective-permute-done.16.mine, bf16[64,1536]{1,0:T(8,128)(2,1)S(1)} %collective-permute-done.17.theirs, bf16[768,1024]{1,0:T(8,128)(2,1)S(1)} %get-tuple-element.32.keys, ...), custom_call_target="tpu_custom_call" | custom-call | flops 301989888 | bytes 655360 | tf_op jit(solution)/shard_map/pallas_call | solution.py:215
  52.8 2.9 %collective-permute-start.18 = (bf16[64,1024]{1,0:T(8,128)(2,1)S(1)}, bf16[64,1024]{1,0:T(8,128)(2,1)S(1)}, u32[]{:S(2)}, u32[]{:S(2)}) collective-permute-start(bf16[64,1024]{1,0:T(8,128)(2,1)S(1)} %get-tuple-element.47), channel_id=1, source_target_pairs={{0,6},{1,7},{2,4},{3,5},{4,2},{5,3},{6,0},{7,1},{8,14},{9,15},{10,... | collective-permute-start | bytes 393224 | tf_op jit(solution)/shard_map/ppermute | solution.py:241
  55.7 2.1 %collective-permute-start.19 = (bf16[64,1024]{1,0:T(8,128)(2,1)S(1)}, bf16[64,1024]{1,0:T(8,128)(2,1)S(1)}, u32[]{:S(2)}, u32[]{:S(2)}) collective-permute-start(bf16[64,1024]{1,0:T(8,128)(2,1)S(1)} %get-tuple-element.48), channel_id=1, source_target_pairs={{0,7},{1,6},{2,5},{3,4},{4,3},{5,2},{6,1},{7,0},{8,15},{9,14},{10,... | collective-permute-start | bytes 393224 | tf_op jit(solution)/shard_map/ppermute | solution.py:241
  57.8 2.5 %shard_map.70 = (bf16[64,1024]{1,0:T(8,128)(2,1)S(1)}, bf16[64,1024]{1,0:T(8,128)(2,1)S(1)}) custom-call(s32[1]{0:T(128)} %bitcast.scal, bf16[64,1536]{1,0:T(8,128)(2,1)S(1)} %collective-permute-done.12.mine, bf16[64,1536]{1,0:T(8,128)(2,1)S(1)} %collective-permute-done.13.theirs, bf16[768,1024]{1,0:T(8,128)(2,1)S(1)} %get-tuple-element.32.keys, ...), custom_call_target="tpu_custom_call" | custom-call | flops 301989888 | bytes 655360 | tf_op jit(solution)/shard_map/pallas_call | solution.py:215
  60.3 5.2 %collective-permute-done.8.mine = bf16[64,1536]{1,0:T(8,128)(2,1)S(1)} collective-permute-done((bf16[64,1536]{1,0:T(8,128)(2,1)S(1)}, bf16[64,1536]{1,0:T(8,128)(2,1)S(1)}, u32[]{:S(2)}, u32[]{:S(2)}) %collective-permute-start.8) | collective-permute-done | bytes 196640 | tf_op jit(solution)/shard_map/ppermute | solution.py:241
  65.6 4.1 %collective-permute-done.9.theirs = bf16[64,1536]{1,0:T(8,128)(2,1)S(1)} collective-permute-done((bf16[64,1536]{1,0:T(8,128)(2,1)S(1)}, bf16[64,1536]{1,0:T(8,128)(2,1)S(1)}, u32[]{:S(2)}, u32[]{:S(2)}) %collective-permute-start.9) | collective-permute-done | bytes 196640 | tf_op jit(solution)/shard_map/ppermute | solution.py:241
  69.9 2.5 %shard_map.69 = (bf16[64,1024]{1,0:T(8,128)(2,1)S(1)}, bf16[64,1024]{1,0:T(8,128)(2,1)S(1)}) custom-call(s32[1]{0:T(128)} %bitcast.scal, bf16[64,1536]{1,0:T(8,128)(2,1)S(1)} %collective-permute-done.8.mine, bf16[64,1536]{1,0:T(8,128)(2,1)S(1)} %collective-permute-done.9.theirs, bf16[768,1024]{1,0:T(8,128)(2,1)S(1)} %get-tuple-element.32.keys, ...), custom_call_target="tpu_custom_call" | custom-call | flops 301989888 | bytes 655360 | tf_op jit(solution)/shard_map/pallas_call | solution.py:215
  72.4 2.2 %collective-permute-start.10 = (bf16[64,1024]{1,0:T(8,128)(2,1)S(1)}, bf16[64,1024]{1,0:T(8,128)(2,1)S(1)}, u32[]{:S(2)}, u32[]{:S(2)}) collective-permute-start(bf16[64,1024]{1,0:T(8,128)(2,1)S(1)} %get-tuple-element.39), channel_id=1, source_target_pairs={{0,2},{1,3},{2,0},{3,1},{4,6},{5,7},{6,4},{7,5},{8,10},{9,11},{10,... | collective-permute-start | bytes 393224 | tf_op jit(solution)/shard_map/ppermute | solution.py:241
  74.6 2.5 %shard_map.68 = (bf16[64,1024]{1,0:T(8,128)(2,1)S(1)}, bf16[64,1024]{1,0:T(8,128)(2,1)S(1)}) custom-call(s32[1]{0:T(128)} %bitcast.scal, bf16[64,1536]{1,0:T(8,128)(2,1)S(1)} %get-tuple-element.27.mine, bf16[64,1536]{1,0:T(8,128)(2,1)S(1)} %collective-permute-done.theirs, bf16[768,1024]{1,0:T(8,128)(2,1)S(1)} %get-tuple-element.32.keys, ...), custom_call_target="tpu_custom_call" | custom-call | flops 301989888 | bytes 655360 | tf_op jit(solution)/shard_map/pallas_call | solution.py:215
  77.8 2.3 %collective-permute-done.15.refs_5_ = bf16[64,1024]{1,0:T(8,128)(2,1)S(1)} collective-permute-done((bf16[64,1024]{1,0:T(8,128)(2,1)S(1)}, bf16[64,1024]{1,0:T(8,128)(2,1)S(1)}, u32[]{:S(2)}, u32[]{:S(2)}) %collective-permute-start.15) | collective-permute-done | bytes 131104 | tf_op jit(solution)/shard_map/ppermute | solution.py:241
  80.1 2.8 %collective-permute-done.10.refs_2_ = bf16[64,1024]{1,0:T(8,128)(2,1)S(1)} collective-permute-done((bf16[64,1024]{1,0:T(8,128)(2,1)S(1)}, bf16[64,1024]{1,0:T(8,128)(2,1)S(1)}, u32[]{:S(2)}, u32[]{:S(2)}) %collective-permute-start.10) | collective-permute-done | bytes 131104 | tf_op jit(solution)/shard_map/ppermute | solution.py:241
  82.9 2.8 %collective-permute-done.11.refs_3_ = bf16[64,1024]{1,0:T(8,128)(2,1)S(1)} collective-permute-done((bf16[64,1024]{1,0:T(8,128)(2,1)S(1)}, bf16[64,1024]{1,0:T(8,128)(2,1)S(1)}, u32[]{:S(2)}, u32[]{:S(2)}) %collective-permute-start.11) | collective-permute-done | bytes 131104 | tf_op jit(solution)/shard_map/ppermute | solution.py:241
  (29 shorter events, 4.8 us)
Async XLA Ops:
  0.0 47.7 %copy-start = (bf16[512,1024]{1,0:T(8,128)(2,1)S(1)}, bf16[512,1024]{1,0:T(8,128)(2,1)}, u32[]{:S(2)}) copy-start(bf16[512,1024]{1,0:T(8,128)(2,1)} %key_weight.1) | copy-start | bytes 3145732
  0.0 47.7 %copy-start.1 = (bf16[512,1024]{1,0:T(8,128)(2,1)S(1)}, bf16[512,1024]{1,0:T(8,128)(2,1)}, u32[]{:S(2)}) copy-start(bf16[512,1024]{1,0:T(8,128)(2,1)} %value_weight.1) | copy-start | bytes 3145732
  2.1 7.9 %collective-permute-start.2 = (bf16[64,640]{1,0:T(8,128)(2,1)S(1)}, bf16[64,640]{1,0:T(8,128)(2,1)S(1)}, u32[]{:S(2)}, u32[]{:S(2)}) collective-permute-start(bf16[64,640]{1,0:T(8,128)(2,1)S(1)} %get-tuple-element.29.refs_0_), channel_id=1, source_target_pairs={{0,4},{1,5},{2,6},{3,7},{4,0},{5,1},{6,2},{7,3},{8,12},{9,13},{10,... | collective-permute-start | bytes 245768 | tf_op jit(solution)/shard_map/ppermute | solution.py:241
  6.2 5.0 %collective-permute-start.1 = (bf16[64,640]{1,0:T(8,128)(2,1)S(1)}, bf16[64,640]{1,0:T(8,128)(2,1)S(1)}, u32[]{:S(2)}, u32[]{:S(2)}) collective-permute-start(bf16[64,640]{1,0:T(8,128)(2,1)S(1)} %get-tuple-element.29.refs_0_), channel_id=1, source_target_pairs={{0,2},{1,3},{2,0},{3,1},{4,6},{5,7},{6,4},{7,5},{8,10},{9,11},{10,... | collective-permute-start | bytes 245768 | tf_op jit(solution)/shard_map/ppermute | solution.py:241
  10.0 4.4 %collective-permute-start.3 = (bf16[64,640]{1,0:T(8,128)(2,1)S(1)}, bf16[64,640]{1,0:T(8,128)(2,1)S(1)}, u32[]{:S(2)}, u32[]{:S(2)}) collective-permute-start(bf16[64,640]{1,0:T(8,128)(2,1)S(1)} %collective-permute-done.2.refs_2_), channel_id=1, source_target_pairs={{0,2},{1,3},{2,0},{3,1},{4,6},{5,7},{6,4},{7,5},{8,10},{9,11},{10,... | collective-permute-start | bytes 245768 | tf_op jit(solution)/shard_map/ppermute | solution.py:241
  14.5 7.6 %collective-permute-start.4 = (bf16[128,640]{1,0:T(8,128)(2,1)S(1)}, bf16[128,640]{1,0:T(8,128)(2,1)S(1)}, u32[]{:S(2)}, u32[]{:S(2)}) collective-permute-start(bf16[128,640]{1,0:T(8,128)(2,1)S(1)} %get-tuple-element.31), channel_id=1, source_target_pairs={{0,8},{8,16},{16,24},{1,9},{9,17},{17,25},{2,10},{10,18},{18,26},{... | collective-permute-start | bytes 491528 | tf_op jit(solution)/shard_map/ppermute | solution.py:285
  18.3 29.3 %collective-permute-start.5 = (bf16[256,640]{1,0:T(8,128)(2,1)S(1)}, bf16[256,640]{1,0:T(8,128)(2,1)S(1)}, u32[]{:S(2)}, u32[]{:S(2)}) collective-permute-start(bf16[256,640]{1,0:T(8,128)(2,1)S(1)} %get-tuple-element.30.own), channel_id=1, source_target_pairs={{0,1},{1,0},{2,3},{3,2},{4,5},{5,4},{6,7},{7,6},{8,9},{9,8},{10,11... | collective-permute-start | bytes 983048 | tf_op jit(solution)/shard_map/ppermute | solution.py:241
  18.4 9.7 %collective-permute-start.16 = (bf16[64,1536]{1,0:T(8,128)(2,1)S(1)}, bf16[64,1536]{1,0:T(8,128)(2,1)S(1)}, u32[]{:S(2)}, u32[]{:S(2)}) collective-permute-start(bf16[64,1536]{1,0:T(8,128)(2,1)S(1)} %get-tuple-element.45), channel_id=1, source_target_pairs={{0,6},{1,7},{2,4},{3,5},{4,2},{5,3},{6,0},{7,1},{8,14},{9,15},{10,... | collective-permute-start | bytes 589832 | tf_op jit(solution)/shard_map/ppermute | solution.py:241
  22.0 19.5 %collective-permute-start.17 = (bf16[64,1536]{1,0:T(8,128)(2,1)S(1)}, bf16[64,1536]{1,0:T(8,128)(2,1)S(1)}, u32[]{:S(2)}, u32[]{:S(2)}) collective-permute-start(bf16[64,1536]{1,0:T(8,128)(2,1)S(1)} %get-tuple-element.46), channel_id=1, source_target_pairs={{0,7},{1,6},{2,5},{3,4},{4,3},{5,2},{6,1},{7,0},{8,15},{9,14},{10,... | collective-permute-start | bytes 589832 | tf_op jit(solution)/shard_map/ppermute | solution.py:241
  22.1 25.5 %collective-permute-start.6 = (bf16[128,640]{1,0:T(8,128)(2,1)S(1)}, bf16[128,640]{1,0:T(8,128)(2,1)S(1)}, u32[]{:S(2)}, u32[]{:S(2)}) collective-permute-start(bf16[128,640]{1,0:T(8,128)(2,1)S(1)} %collective-permute-done.4.earlier), channel_id=1, source_target_pairs={{0,1},{1,0},{2,3},{3,2},{4,5},{5,4},{6,7},{7,6},{8,9},{9,8},{10,11... | collective-permute-start | bytes 491528 | tf_op jit(solution)/shard_map/ppermute | solution.py:241
  22.4 30.4 %collective-permute-start.12 = (bf16[64,1536]{1,0:T(8,128)(2,1)S(1)}, bf16[64,1536]{1,0:T(8,128)(2,1)S(1)}, u32[]{:S(2)}, u32[]{:S(2)}) collective-permute-start(bf16[64,1536]{1,0:T(8,128)(2,1)S(1)} %get-tuple-element.41), channel_id=1, source_target_pairs={{0,4},{1,5},{2,6},{3,7},{4,0},{5,1},{6,2},{7,3},{8,12},{9,13},{10,... | collective-permute-start | bytes 589832 | tf_op jit(solution)/shard_map/ppermute | solution.py:241
  28.1 27.6 %collective-permute-start.13 = (bf16[64,1536]{1,0:T(8,128)(2,1)S(1)}, bf16[64,1536]{1,0:T(8,128)(2,1)S(1)}, u32[]{:S(2)}, u32[]{:S(2)}) collective-permute-start(bf16[64,1536]{1,0:T(8,128)(2,1)S(1)} %get-tuple-element.42), channel_id=1, source_target_pairs={{0,5},{1,4},{2,7},{3,6},{4,1},{5,0},{6,3},{7,2},{8,13},{9,12},{10,... | collective-permute-start | bytes 589832 | tf_op jit(solution)/shard_map/ppermute | solution.py:241
  41.6 23.9 %collective-permute-start.8 = (bf16[64,1536]{1,0:T(8,128)(2,1)S(1)}, bf16[64,1536]{1,0:T(8,128)(2,1)S(1)}, u32[]{:S(2)}, u32[]{:S(2)}) collective-permute-start(bf16[64,1536]{1,0:T(8,128)(2,1)S(1)} %get-tuple-element.37), channel_id=1, source_target_pairs={{0,2},{1,3},{2,0},{3,1},{4,6},{5,7},{6,4},{7,5},{8,10},{9,11},{10,... | collective-permute-start | bytes 589832 | tf_op jit(solution)/shard_map/ppermute | solution.py:241
  47.5 22.1 %collective-permute-start.9 = (bf16[64,1536]{1,0:T(8,128)(2,1)S(1)}, bf16[64,1536]{1,0:T(8,128)(2,1)S(1)}, u32[]{:S(2)}, u32[]{:S(2)}) collective-permute-start(bf16[64,1536]{1,0:T(8,128)(2,1)S(1)} %get-tuple-element.38), channel_id=1, source_target_pairs={{0,3},{1,2},{2,1},{3,0},{4,7},{5,6},{6,5},{7,4},{8,11},{9,10},{10,... | collective-permute-start | bytes 589832 | tf_op jit(solution)/shard_map/ppermute | solution.py:241
  47.6 24.9 %collective-permute-start = (bf16[64,1536]{1,0:T(8,128)(2,1)S(1)}, bf16[64,1536]{1,0:T(8,128)(2,1)S(1)}, u32[]{:S(2)}, u32[]{:S(2)}) collective-permute-start(bf16[64,1536]{1,0:T(8,128)(2,1)S(1)} %get-tuple-element.28), channel_id=1, source_target_pairs={{0,1},{1,0},{2,3},{3,2},{4,5},{5,4},{6,7},{7,6},{8,9},{9,8},{10,11... | collective-permute-start | bytes 589832 | tf_op jit(solution)/shard_map/ppermute | solution.py:241
  52.8 24.4 %collective-permute-start.18 = (bf16[64,1024]{1,0:T(8,128)(2,1)S(1)}, bf16[64,1024]{1,0:T(8,128)(2,1)S(1)}, u32[]{:S(2)}, u32[]{:S(2)}) collective-permute-start(bf16[64,1024]{1,0:T(8,128)(2,1)S(1)} %get-tuple-element.47), channel_id=1, source_target_pairs={{0,6},{1,7},{2,4},{3,5},{4,2},{5,3},{6,0},{7,1},{8,14},{9,15},{10,... | collective-permute-start | bytes 393224 | tf_op jit(solution)/shard_map/ppermute | solution.py:241
  55.7 21.9 %collective-permute-start.19 = (bf16[64,1024]{1,0:T(8,128)(2,1)S(1)}, bf16[64,1024]{1,0:T(8,128)(2,1)S(1)}, u32[]{:S(2)}, u32[]{:S(2)}) collective-permute-start(bf16[64,1024]{1,0:T(8,128)(2,1)S(1)} %get-tuple-element.48), channel_id=1, source_target_pairs={{0,7},{1,6},{2,5},{3,4},{4,3},{5,2},{6,1},{7,0},{8,15},{9,14},{10,... | collective-permute-start | bytes 393224 | tf_op jit(solution)/shard_map/ppermute | solution.py:241
  65.5 12.3 %collective-permute-start.14 = (bf16[64,1024]{1,0:T(8,128)(2,1)S(1)}, bf16[64,1024]{1,0:T(8,128)(2,1)S(1)}, u32[]{:S(2)}, u32[]{:S(2)}) collective-permute-start(bf16[64,1024]{1,0:T(8,128)(2,1)S(1)} %get-tuple-element.43), channel_id=1, source_target_pairs={{0,4},{1,5},{2,6},{3,7},{4,0},{5,1},{6,2},{7,3},{8,12},{9,13},{10,... | collective-permute-start | bytes 393224 | tf_op jit(solution)/shard_map/ppermute | solution.py:241
  69.7 10.4 %collective-permute-start.15 = (bf16[64,1024]{1,0:T(8,128)(2,1)S(1)}, bf16[64,1024]{1,0:T(8,128)(2,1)S(1)}, u32[]{:S(2)}, u32[]{:S(2)}) collective-permute-start(bf16[64,1024]{1,0:T(8,128)(2,1)S(1)} %get-tuple-element.44), channel_id=1, source_target_pairs={{0,5},{1,4},{2,7},{3,6},{4,1},{5,0},{6,3},{7,2},{8,13},{9,12},{10,... | collective-permute-start | bytes 393224 | tf_op jit(solution)/shard_map/ppermute | solution.py:241
  72.4 10.5 %collective-permute-start.10 = (bf16[64,1024]{1,0:T(8,128)(2,1)S(1)}, bf16[64,1024]{1,0:T(8,128)(2,1)S(1)}, u32[]{:S(2)}, u32[]{:S(2)}) collective-permute-start(bf16[64,1024]{1,0:T(8,128)(2,1)S(1)} %get-tuple-element.39), channel_id=1, source_target_pairs={{0,2},{1,3},{2,0},{3,1},{4,6},{5,7},{6,4},{7,5},{8,10},{9,11},{10,... | collective-permute-start | bytes 393224 | tf_op jit(solution)/shard_map/ppermute | solution.py:241
  77.2 8.5 %collective-permute-start.11 = (bf16[64,1024]{1,0:T(8,128)(2,1)S(1)}, bf16[64,1024]{1,0:T(8,128)(2,1)S(1)}, u32[]{:S(2)}, u32[]{:S(2)}) collective-permute-start(bf16[64,1024]{1,0:T(8,128)(2,1)S(1)} %get-tuple-element.40), channel_id=1, source_target_pairs={{0,3},{1,2},{2,1},{3,0},{4,7},{5,6},{6,5},{7,4},{8,11},{9,10},{10,... | collective-permute-start | bytes 393224 | tf_op jit(solution)/shard_map/ppermute | solution.py:241
  77.6 8.1 %collective-permute-start.7 = (bf16[64,1024]{1,0:T(8,128)(2,1)S(1)}, bf16[64,1024]{1,0:T(8,128)(2,1)S(1)}, u32[]{:S(2)}, u32[]{:S(2)}) collective-permute-start(bf16[64,1024]{1,0:T(8,128)(2,1)S(1)} %get-tuple-element.36), channel_id=1, source_target_pairs={{0,1},{1,0},{2,3},{3,2},{4,5},{5,4},{6,7},{7,6},{8,9},{9,8},{10,11... | collective-permute-start | bytes 393224 | tf_op jit(solution)/shard_map/ppermute | solution.py:241
